TPU v7x, 32 devices: a whole 2x2x4 slice. The times are simulated.
32 devices in a mesh: group: 4 (over y, x), dom: 8 (over z, core).
Axes of the slice: x: 2, y: 2, z: 4, core: 2. Of those that a mesh axis runs over, the one named last changes fastest.
Arguments:
- p_start: float32 [1024, 128], P(('group', 'dom')), may hold values from -60 to 60
- r_start: float32 [1024, 128], P(('group', 'dom')), may hold values from -60 to 60
- diag_shift: float32 [1024, 128], P(('group', 'dom')), may hold values from 0.5 to 2
- shifts: float32 [8], replicated, may hold values from 0.5 to 1.5
- block_values: float32 [1024, 6, 128, 128], P(('group', 'dom')), may hold values from -0.21875 to 0.21875
- block_cols: int32 [1024, 6], P(('group', 'dom')), may hold values from 0 to 95, as said below
- live_slots: int32 [1024], P(('group', 'dom')), may hold values from 2 to 6, as said below
- needed: int32 [32, 4, 16], P(('group', 'dom')), may hold values from 0 to 31
Outputs:
- basis: float32 [17, 1024, 128], P(None, ('group', 'dom'))
- gram: float32 [17, 17], replicated
Inputs may be any that keep to these rules, and one draw needn't show every extreme that they name: `block_cols`: slot 0 of block row b is the row itself (b mod 32); a value below 32 names a block row of the same device, a value 32 + k * 16 + h names entry h of the device's list k of needed. Devices with dom index 0 never use list 0 in used slots, devices with the last dom index never list 1. Slots from live_slots on hold values in range but are not used. `live_slots`: the first block row of every device uses all 6 slots. needed[d, k] lists the local block rows that device d reads from its source s_k(d), in the order of its extended field.
All inputs are finite; a program needn't handle non-finite values.
Results may differ from a plain program's by a relative error of at most 0.0001.
Values sent between devices are 32-bit elements; how exact they have to be, the bound alone decides.
No kernel may reach another device: no remote copies, remote signals or barrier semaphores. Data moves between devices by JAX's collectives and lax.ppermute only.
A program may use at most 64 MiB of HBM per device.

v0:
```python
import functools
import jax
import jax.numpy as jnp
from jax import lax
from jax.experimental import pallas as pl
from jax.experimental.pallas import tpu as pltpu
from jax.sharding import PartitionSpec as P

def table_kernel(cols, live, need, tbl, *, rows, nslots, halo):
    far = 10 * rows

    def build(b, carry):
        n = live[b]
        for s in range(nslots):
            c = cols[b, s]
            local = c < rows
            q = jnp.maximum(c - rows, 0)
            k = q // halo
            row = jnp.where(local, c, 2 * rows * (k + 1) + need[k, q % halo])
            tbl[b * nslots + s] = jnp.where(s < n, row, far)
        return carry

    lax.fori_loop(0, rows, build, 0)


def step_kernel(tbl, shifts, cur, diag, h0, h1, h2, h3, a_ref, out, ext, halves, *, step, rows, nslots):
    bs = ext.shape[1]
    half = bs // 2
    far = 10 * rows
    for k, h in enumerate((cur, h0, h1, h2, h3)):
        ext[2 * rows * k : 2 * rows * (k + 1), :] = h[...]
    ext[far:, :] = jnp.zeros((ext.shape[0] - far, bs), jnp.float32)
    halves[...] = jnp.zeros(halves.shape, halves.dtype)
    low = lax.broadcasted_iota(jnp.int32, (bs, bs), 1) < half
    r = lax.broadcasted_iota(jnp.int32, (8, 2 * bs), 0)
    c = lax.broadcasted_iota(jnp.int32, (8, 2 * bs), 1) % bs
    pick = (((r == 0) & (c < half)) | ((r == 1) & (c >= half))).astype(jnp.float32).astype(jnp.bfloat16)

    def lane_sums(at):
        sums = lax.dot_general(
            pick, halves[...], (((1,), (1,)), ((), ())), preferred_element_type=jnp.float32
        )
        for u in range(2):
            out[pl.ds(at + u, 1), :] = sums[0:1, u * bs : (u + 1) * bs]
            out[pl.ds(rows + at + u, 1), :] = sums[1:2, u * bs : (u + 1) * bs]

    def pair(g, carry):
        lane_sums(jnp.maximum(2 * g - 2, 0))
        for u in range(2):
            first = (2 * g + u) * nslots
            ap = ar = None
            for s in range(nslots):
                at = tbl[first + s]
                a = a_ref[first + s]
                tp = a * ext[pl.ds(at, 1), :]
                tr = a * ext[pl.ds(at + rows, 1), :]
                ap = tp if ap is None else ap + tp
                ar = tr if ar is None else ar + tr
            both = jnp.where(low, ap + pltpu.roll(ap, half, 1), ar + pltpu.roll(ar, half, 1))
            hi = both.astype(jnp.bfloat16)
            lo = (both - hi.astype(jnp.float32)).astype(jnp.bfloat16)
            halves[u * bs : (u + 1) * bs, 0:bs] = hi
            halves[u * bs : (u + 1) * bs, bs:] = lo
        return carry

    lax.fori_loop(0, rows // 2, pair, 0)
    lane_sums(rows - 2)
    d = diag[...] - shifts[step]
    out[0:rows, :] += d * cur[0:rows, :]
    out[rows : 2 * rows, :] += d * cur[rows : 2 * rows, :]


def sum_over(x, axis):
    n = lax.axis_size(axis)
    if n & (n - 1):
        return lax.psum(x, axis)
    d = 1
    while d < n:
        x = x + lax.ppermute(x, axis, [(i, i ^ d) for i in range(n)])
        d *= 2
    return x


def per_device(p_start, r_start, diag_shift, shifts, block_values, block_cols, live_slots, needed):
    rows, bs = p_start.shape
    nslots = block_values.shape[1]
    halo = needed.shape[2]
    depth = shifts.shape[0]
    f32 = jnp.float32
    smem = pl.BlockSpec(memory_space=pltpu.SMEM)
    vmem = pl.BlockSpec(memory_space=pltpu.VMEM)
    field = jax.ShapeDtypeStruct((2 * rows, bs), f32)
    scratch = [pltpu.VMEM((10 * rows + rows + 8, bs), f32), pltpu.VMEM((2 * bs, 2 * bs), jnp.bfloat16)]
    params = pltpu.CompilerParams(vmem_limit_bytes=24 * 1024 * 1024)
    a_flat = block_values.reshape(rows * nslots, bs, bs)
    tbl = pl.pallas_call(
        functools.partial(table_kernel, rows=rows, nslots=nslots, halo=halo),
        out_shape=jax.ShapeDtypeStruct((rows * nslots,), jnp.int32),
        in_specs=[smem, smem, smem],
        out_specs=smem,
        name="table",
    )(block_cols, live_slots, needed[0])

    def halos(cur):
        nd, ng = lax.axis_size("dom"), lax.axis_size("group")
        up = [(i, (i + 1) % nd) for i in range(nd)]
        down = [((i + 1) % nd, i) for i in range(nd)]
        gup = [(i, (i + 1) % ng) for i in range(ng)]
        gdown = [((i + 1) % ng, i) for i in range(ng)]
        return (
            lax.ppermute(cur, "dom", up),
            lax.ppermute(cur, "dom", down),
            lax.ppermute(cur, "group", gup),
            lax.ppermute(cur, "group", gdown),
        )

    cur = jnp.concatenate([p_start, r_start], axis=0)
    fields = [cur]
    for step in range(depth):
        h = halos(cur)
        cur = pl.pallas_call(
            functools.partial(step_kernel, step=step, rows=rows, nslots=nslots),
            out_shape=field,
            in_specs=[smem, smem] + [vmem] * 7,
            out_specs=vmem,
            scratch_shapes=scratch,
            compiler_params=params,
            name="step",
        )(tbl, shifts, cur, diag_shift, *h, a_flat)
        fields.append(cur)
    both = jnp.stack(fields).reshape(depth + 1, 2, rows, bs)
    basis = jnp.concatenate([both[:, 0], both[:depth, 1]], axis=0)
    total_cells = rows * bs * lax.axis_size("group") * lax.axis_size("dom")
    local_gram = jnp.einsum("kbi,lbi->kl", basis, basis, precision=lax.Precision.HIGHEST)
    return basis, sum_over(sum_over(local_gram, "dom"), "group") / total_cells


def solution(mesh):
    return jax.shard_map(
        per_device,
        mesh=mesh,
        in_specs=(
            P(("group", "dom"), None),
            P(("group", "dom"), None),
            P(("group", "dom"), None),
            P(),
            P(("group", "dom"), None, None, None),
            P(("group", "dom"), None),
            P(("group", "dom")),
            P(("group", "dom"), None, None),
        ),
        out_specs=(P(None, ("group", "dom"), None), P()),
        check_vma=False,
    )
```

profile of v0, /device:TPU:0, one launch (start us, length us, event | category | flops | bytes accessed | tf_op | source)
XLA Modules:
  0.0 134.3 jit_solution(11907063971673150591)
XLA Ops:
  2.1 3.9 %collective-permute-start.3 = (f32[64,128]{1,0:T(8,128)S(1)}, f32[64,128]{1,0:T(8,128)S(1)}, u32[]{:S(2)}, u32[]{:S(2)}) collective-permute-start(f32[64,128]{1,0:T(8,128)S(1)} %constant_dynamic-update-slice_fusion.cur), channel_id=1, source_target_pairs={{8,0},{16,8},{24,16},{0,24},{9,1},{17,9},{25,17},{1,25},{10,2},{18... | collective-permute-start | bytes 98312 | tf_op jit(solution)/shard_map/ppermute | solution.py:114
  10.1 3.1 %table.1.tbl = s32[192]{0:T(256)} custom-call(s32[32,6]{1,0:T(8,128)} %copy.10.cols, s32[32]{0:T(128)} %live.1, s32[4,16]{1,0:T(4,128)} %bitcast.68), custom_call_target="tpu_custom_call" | custom-call | tf_op jit(solution)/shard_map/table/pallas_call | solution.py:96
  13.9 4.6 %copy-done = f32[32,6,128,128]{3,2,1,0:T(8,128)S(1)} copy-done((f32[32,6,128,128]{3,2,1,0:T(8,128)S(1)}, f32[32,6,128,128]{3,2,1,0:T(8,128)}, u32[]{:S(2)}) %copy-start) | copy-done | bytes 12582936
  20.5 4.0 %step.8.cur = f32[64,128]{1,0:T(8,128)S(1)} custom-call(s32[192]{0:T(256)S(1)} %copy-done.5, f32[8]{0:T(128)S(1)} %copy-done.7, f32[64,128]{1,0:T(8,128)S(1)} %constant_dynamic-update-slice_fusion.cur, f32[32,128]{1,0:T(8,128)S(1)} %copy-done.3, f32[64,128]{1,0:T(8,128)S(1)} %collective-permute-done.h0, f32[64,128]{1,0:T(8,128)S(1)} %collective-permute-done.1.h1, ...), custom_call_target="tpu_custom_call" | custom-call | tf_op jit(solution)/shard_map/step/pallas_call | solution.py:121
  32.0 3.0 %collective-permute-done.4.h0 = f32[64,128]{1,0:T(8,128)S(1)} collective-permute-done((f32[64,128]{1,0:T(8,128)S(1)}, f32[64,128]{1,0:T(8,128)S(1)}, u32[]{:S(2)}, u32[]{:S(2)}) %collective-permute-start.4) | collective-permute-done | bytes 32800 | tf_op jit(solution)/shard_map/ppermute | solution.py:111
  35.0 4.0 %step.9.cur = f32[64,128]{1,0:T(8,128)S(1)} custom-call(s32[192]{0:T(256)S(1)} %copy-done.5, f32[8]{0:T(128)S(1)} %copy-done.7, f32[64,128]{1,0:T(8,128)S(1)} %step.8.cur, f32[32,128]{1,0:T(8,128)S(1)} %copy-done.3, f32[64,128]{1,0:T(8,128)S(1)} %collective-permute-done.4.h0, f32[64,128]{1,0:T(8,128)S(1)} %collective-permute-done.5.h1, ...), custom_call_target="tpu_custom_call" | custom-call | tf_op jit(solution)/shard_map/step/pallas_call | solution.py:121
  43.2 3.2 %collective-permute-done.10.h2 = f32[64,128]{1,0:T(8,128)S(1)} collective-permute-done((f32[64,128]{1,0:T(8,128)S(1)}, f32[64,128]{1,0:T(8,128)S(1)}, u32[]{:S(2)}, u32[]{:S(2)}) %collective-permute-start.10) | collective-permute-done | bytes 32800 | tf_op jit(solution)/shard_map/ppermute | solution.py:113
  46.8 4.0 %step.10.cur = f32[64,128]{1,0:T(8,128)S(1)} custom-call(s32[192]{0:T(256)S(1)} %copy-done.5, f32[8]{0:T(128)S(1)} %copy-done.7, f32[64,128]{1,0:T(8,128)S(1)} %step.9.cur, f32[32,128]{1,0:T(8,128)S(1)} %copy-done.3, f32[64,128]{1,0:T(8,128)S(1)} %collective-permute-done.8.h0, f32[64,128]{1,0:T(8,128)S(1)} %collective-permute-done.9.h1, ...), custom_call_target="tpu_custom_call" | custom-call | tf_op jit(solution)/shard_map/step/pallas_call | solution.py:121
  50.7 3.0 %collective-permute-start.15 = (f32[64,128]{1,0:T(8,128)S(1)}, f32[64,128]{1,0:T(8,128)S(1)}, u32[]{:S(2)}, u32[]{:S(2)}) collective-permute-start(f32[64,128]{1,0:T(8,128)S(1)} %step.10.cur), channel_id=1, source_target_pairs={{8,0},{16,8},{24,16},{0,24},{9,1},{17,9},{25,17},{1,25},{10,2},{18... | collective-permute-start | bytes 98312 | tf_op jit(solution)/shard_map/ppermute | solution.py:114
  55.3 3.2 %collective-permute-done.14.h2 = f32[64,128]{1,0:T(8,128)S(1)} collective-permute-done((f32[64,128]{1,0:T(8,128)S(1)}, f32[64,128]{1,0:T(8,128)S(1)}, u32[]{:S(2)}, u32[]{:S(2)}) %collective-permute-start.14) | collective-permute-done | bytes 32800 | tf_op jit(solution)/shard_map/ppermute | solution.py:113
  58.8 4.0 %step.11.cur = f32[64,128]{1,0:T(8,128)S(1)} custom-call(s32[192]{0:T(256)S(1)} %copy-done.5, f32[8]{0:T(128)S(1)} %copy-done.7, f32[64,128]{1,0:T(8,128)S(1)} %step.10.cur, f32[32,128]{1,0:T(8,128)S(1)} %copy-done.3, f32[64,128]{1,0:T(8,128)S(1)} %collective-permute-done.12.h0, f32[64,128]{1,0:T(8,128)S(1)} %collective-permute-done.13.h1, ...), custom_call_target="tpu_custom_call" | custom-call | tf_op jit(solution)/shard_map/step/pallas_call | solution.py:121
  62.8 3.0 %collective-permute-start.19 = (f32[64,128]{1,0:T(8,128)S(1)}, f32[64,128]{1,0:T(8,128)S(1)}, u32[]{:S(2)}, u32[]{:S(2)}) collective-permute-start(f32[64,128]{1,0:T(8,128)S(1)} %step.11.cur), channel_id=1, source_target_pairs={{8,0},{16,8},{24,16},{0,24},{9,1},{17,9},{25,17},{1,25},{10,2},{18... | collective-permute-start | bytes 98312 | tf_op jit(solution)/shard_map/ppermute | solution.py:114
  67.4 3.2 %collective-permute-done.18.h2 = f32[64,128]{1,0:T(8,128)S(1)} collective-permute-done((f32[64,128]{1,0:T(8,128)S(1)}, f32[64,128]{1,0:T(8,128)S(1)}, u32[]{:S(2)}, u32[]{:S(2)}) %collective-permute-start.18) | collective-permute-done | bytes 32800 | tf_op jit(solution)/shard_map/ppermute | solution.py:113
  70.9 4.0 %step.12.cur = f32[64,128]{1,0:T(8,128)S(1)} custom-call(s32[192]{0:T(256)S(1)} %copy-done.5, f32[8]{0:T(128)S(1)} %copy-done.7, f32[64,128]{1,0:T(8,128)S(1)} %step.11.cur, f32[32,128]{1,0:T(8,128)S(1)} %copy-done.3, f32[64,128]{1,0:T(8,128)S(1)} %collective-permute-done.16.h0, f32[64,128]{1,0:T(8,128)S(1)} %collective-permute-done.17.h1, ...), custom_call_target="tpu_custom_call" | custom-call | tf_op jit(solution)/shard_map/step/pallas_call | solution.py:121
  74.9 3.0 %collective-permute-start.23 = (f32[64,128]{1,0:T(8,128)S(1)}, f32[64,128]{1,0:T(8,128)S(1)}, u32[]{:S(2)}, u32[]{:S(2)}) collective-permute-start(f32[64,128]{1,0:T(8,128)S(1)} %step.12.cur), channel_id=1, source_target_pairs={{8,0},{16,8},{24,16},{0,24},{9,1},{17,9},{25,17},{1,25},{10,2},{18... | collective-permute-start | bytes 98312 | tf_op jit(solution)/shard_map/ppermute | solution.py:114
  79.5 3.2 %collective-permute-done.22.h2 = f32[64,128]{1,0:T(8,128)S(1)} collective-permute-done((f32[64,128]{1,0:T(8,128)S(1)}, f32[64,128]{1,0:T(8,128)S(1)}, u32[]{:S(2)}, u32[]{:S(2)}) %collective-permute-start.22) | collective-permute-done | bytes 32800 | tf_op jit(solution)/shard_map/ppermute | solution.py:113
  83.1 4.0 %step.13.cur = f32[64,128]{1,0:T(8,128)S(1)} custom-call(s32[192]{0:T(256)S(1)} %copy-done.5, f32[8]{0:T(128)S(1)} %copy-done.7, f32[64,128]{1,0:T(8,128)S(1)} %step.12.cur, f32[32,128]{1,0:T(8,128)S(1)} %copy-done.3, f32[64,128]{1,0:T(8,128)S(1)} %collective-permute-done.20.h0, f32[64,128]{1,0:T(8,128)S(1)} %collective-permute-done.21.h1, ...), custom_call_target="tpu_custom_call" | custom-call | tf_op jit(solution)/shard_map/step/pallas_call | solution.py:121
  91.6 3.2 %collective-permute-done.26.h2 = f32[64,128]{1,0:T(8,128)S(1)} collective-permute-done((f32[64,128]{1,0:T(8,128)S(1)}, f32[64,128]{1,0:T(8,128)S(1)}, u32[]{:S(2)}, u32[]{:S(2)}) %collective-permute-start.26) | collective-permute-done | bytes 32800 | tf_op jit(solution)/shard_map/ppermute | solution.py:113
  95.1 4.0 %step.14.cur = f32[64,128]{1,0:T(8,128)S(1)} custom-call(s32[192]{0:T(256)S(1)} %copy-done.5, f32[8]{0:T(128)S(1)} %copy-done.7, f32[64,128]{1,0:T(8,128)S(1)} %step.13.cur, f32[32,128]{1,0:T(8,128)S(1)} %copy-done.3, f32[64,128]{1,0:T(8,128)S(1)} %collective-permute-done.24.h0, f32[64,128]{1,0:T(8,128)S(1)} %collective-permute-done.25.h1, ...), custom_call_target="tpu_custom_call" | custom-call | tf_op jit(solution)/shard_map/step/pallas_call | solution.py:121
  103.7 3.2 %collective-permute-done.30.h2 = f32[64,128]{1,0:T(8,128)S(1)} collective-permute-done((f32[64,128]{1,0:T(8,128)S(1)}, f32[64,128]{1,0:T(8,128)S(1)}, u32[]{:S(2)}, u32[]{:S(2)}) %collective-permute-start.30) | collective-permute-done | bytes 32800 | tf_op jit(solution)/shard_map/ppermute | solution.py:113
  107.2 4.6 %copy-done.2 = f32[32,6,128,128]{3,2,1,0:T(8,128)S(1)} copy-done((f32[32,6,128,128]{3,2,1,0:T(8,128)S(1)}, f32[32,6,128,128]{3,2,1,0:T(8,128)}, u32[]{:S(2)}) %copy-start.2) | copy-done | bytes 12582936
  111.8 4.0 %step.15 = f32[64,128]{1,0:T(8,128)S(1)} custom-call(s32[192]{0:T(256)S(1)} %copy-done.6, f32[8]{0:T(128)S(1)} %copy-done.8, f32[64,128]{1,0:T(8,128)S(1)} %step.14.cur, f32[32,128]{1,0:T(8,128)S(1)} %copy-done.4, f32[64,128]{1,0:T(8,128)S(1)} %collective-permute-done.28.h0, f32[64,128]{1,0:T(8,128)S(1)} %collective-permute-done.29.h1, ...), custom_call_target="tpu_custom_call" | custom-call | tf_op jit(solution)/shard_map/step/pallas_call | solution.py:121
  118.0 3.7 %collective-permute-done.33 = f32[17,17]{1,0:T(8,128)S(1)} collective-permute-done((f32[17,17]{1,0:T(8,128)S(1)}, f32[17,17]{1,0:T(8,128)S(1)}, u32[]{:S(2)}, u32[]{:S(2)}) %collective-permute-start.33) | collective-permute-done | bytes 1188 | tf_op jit(solution)/shard_map/ppermute | solution.py:79
  121.7 4.6 %collective-permute-done.34 = f32[17,17]{1,0:T(8,128)S(1)} collective-permute-done((f32[17,17]{1,0:T(8,128)S(1)}, f32[17,17]{1,0:T(8,128)S(1)}, u32[]{:S(2)}, u32[]{:S(2)}) %collective-permute-start.34) | collective-permute-done | bytes 1188 | tf_op jit(solution)/shard_map/ppermute | solution.py:79
  (92 shorter events, 46.1 us)
Async XLA Ops:
  2.1 11.2 %collective-permute-start.3 = (f32[64,128]{1,0:T(8,128)S(1)}, f32[64,128]{1,0:T(8,128)S(1)}, u32[]{:S(2)}, u32[]{:S(2)}) collective-permute-start(f32[64,128]{1,0:T(8,128)S(1)} %constant_dynamic-update-slice_fusion.cur), channel_id=1, source_target_pairs={{8,0},{16,8},{24,16},{0,24},{9,1},{17,9},{25,17},{1,25},{10,2},{18... | collective-permute-start | bytes 98312 | tf_op jit(solution)/shard_map/ppermute | solution.py:114
  6.0 7.3 %collective-permute-start.2 = (f32[64,128]{1,0:T(8,128)S(1)}, f32[64,128]{1,0:T(8,128)S(1)}, u32[]{:S(2)}, u32[]{:S(2)}) collective-permute-start(f32[64,128]{1,0:T(8,128)S(1)} %constant_dynamic-update-slice_fusion.cur), channel_id=1, source_target_pairs={{0,8},{8,16},{16,24},{24,0},{1,9},{9,17},{17,25},{25,1},{2,10},{10... | collective-permute-start | bytes 98312 | tf_op jit(solution)/shard_map/ppermute | solution.py:113
  6.0 7.3 %collective-permute-start.1 = (f32[64,128]{1,0:T(8,128)S(1)}, f32[64,128]{1,0:T(8,128)S(1)}, u32[]{:S(2)}, u32[]{:S(2)}) collective-permute-start(f32[64,128]{1,0:T(8,128)S(1)} %constant_dynamic-update-slice_fusion.cur), channel_id=1, source_target_pairs={{1,0},{2,1},{3,2},{4,3},{5,4},{6,5},{7,6},{0,7},{9,8},{10,9},{11,1... | collective-permute-start | bytes 98312 | tf_op jit(solution)/shard_map/ppermute | solution.py:112
  8.8 5.1 %collective-permute-start = (f32[64,128]{1,0:T(8,128)S(1)}, f32[64,128]{1,0:T(8,128)S(1)}, u32[]{:S(2)}, u32[]{:S(2)}) collective-permute-start(f32[64,128]{1,0:T(8,128)S(1)} %constant_dynamic-update-slice_fusion.cur), channel_id=1, source_target_pairs={{0,1},{1,2},{2,3},{3,4},{4,5},{5,6},{6,7},{7,0},{8,9},{9,10},{10,1... | collective-permute-start | bytes 98312 | tf_op jit(solution)/shard_map/ppermute | solution.py:111
  24.5 5.3 %collective-permute-start.7 = (f32[64,128]{1,0:T(8,128)S(1)}, f32[64,128]{1,0:T(8,128)S(1)}, u32[]{:S(2)}, u32[]{:S(2)}) collective-permute-start(f32[64,128]{1,0:T(8,128)S(1)} %step.8.cur), channel_id=1, source_target_pairs={{8,0},{16,8},{24,16},{0,24},{9,1},{17,9},{25,17},{1,25},{10,2},{18... | collective-permute-start | bytes 98312 | tf_op jit(solution)/shard_map/ppermute | solution.py:114
  27.2 4.8 %collective-permute-start.6 = (f32[64,128]{1,0:T(8,128)S(1)}, f32[64,128]{1,0:T(8,128)S(1)}, u32[]{:S(2)}, u32[]{:S(2)}) collective-permute-start(f32[64,128]{1,0:T(8,128)S(1)} %step.8.cur), channel_id=1, source_target_pairs={{0,8},{8,16},{16,24},{24,0},{1,9},{9,17},{17,25},{25,1},{2,10},{10... | collective-permute-start | bytes 98312 | tf_op jit(solution)/shard_map/ppermute | solution.py:113
  27.2 4.8 %collective-permute-start.5 = (f32[64,128]{1,0:T(8,128)S(1)}, f32[64,128]{1,0:T(8,128)S(1)}, u32[]{:S(2)}, u32[]{:S(2)}) collective-permute-start(f32[64,128]{1,0:T(8,128)S(1)} %step.8.cur), channel_id=1, source_target_pairs={{1,0},{2,1},{3,2},{4,3},{5,4},{6,5},{7,6},{0,7},{9,8},{10,9},{11,1... | collective-permute-start | bytes 98312 | tf_op jit(solution)/shard_map/ppermute | solution.py:112
  29.8 5.1 %collective-permute-start.4 = (f32[64,128]{1,0:T(8,128)S(1)}, f32[64,128]{1,0:T(8,128)S(1)}, u32[]{:S(2)}, u32[]{:S(2)}) collective-permute-start(f32[64,128]{1,0:T(8,128)S(1)} %step.8.cur), channel_id=1, source_target_pairs={{0,1},{1,2},{2,3},{3,4},{4,5},{5,6},{6,7},{7,0},{8,9},{9,10},{10,1... | collective-permute-start | bytes 98312 | tf_op jit(solution)/shard_map/ppermute | solution.py:111
  41.6 4.8 %collective-permute-start.10 = (f32[64,128]{1,0:T(8,128)S(1)}, f32[64,128]{1,0:T(8,128)S(1)}, u32[]{:S(2)}, u32[]{:S(2)}) collective-permute-start(f32[64,128]{1,0:T(8,128)S(1)} %step.9.cur), channel_id=1, source_target_pairs={{0,8},{8,16},{16,24},{24,0},{1,9},{9,17},{17,25},{25,1},{2,10},{10... | collective-permute-start | bytes 98312 | tf_op jit(solution)/shard_map/ppermute | solution.py:113
  41.6 4.8 %collective-permute-start.9 = (f32[64,128]{1,0:T(8,128)S(1)}, f32[64,128]{1,0:T(8,128)S(1)}, u32[]{:S(2)}, u32[]{:S(2)}) collective-permute-start(f32[64,128]{1,0:T(8,128)S(1)} %step.9.cur), channel_id=1, source_target_pairs={{1,0},{2,1},{3,2},{4,3},{5,4},{6,5},{7,6},{0,7},{9,8},{10,9},{11,1... | collective-permute-start | bytes 98312 | tf_op jit(solution)/shard_map/ppermute | solution.py:112
  41.6 5.1 %collective-permute-start.8 = (f32[64,128]{1,0:T(8,128)S(1)}, f32[64,128]{1,0:T(8,128)S(1)}, u32[]{:S(2)}, u32[]{:S(2)}) collective-permute-start(f32[64,128]{1,0:T(8,128)S(1)} %step.9.cur), channel_id=1, source_target_pairs={{0,1},{1,2},{2,3},{3,4},{4,5},{5,6},{6,7},{7,0},{8,9},{9,10},{10,1... | collective-permute-start | bytes 98312 | tf_op jit(solution)/shard_map/ppermute | solution.py:111
  53.7 4.8 %collective-permute-start.14 = (f32[64,128]{1,0:T(8,128)S(1)}, f32[64,128]{1,0:T(8,128)S(1)}, u32[]{:S(2)}, u32[]{:S(2)}) collective-permute-start(f32[64,128]{1,0:T(8,128)S(1)} %step.10.cur), channel_id=1, source_target_pairs={{0,8},{8,16},{16,24},{24,0},{1,9},{9,17},{17,25},{25,1},{2,10},{10... | collective-permute-start | bytes 98312 | tf_op jit(solution)/shard_map/ppermute | solution.py:113
  53.7 4.8 %collective-permute-start.13 = (f32[64,128]{1,0:T(8,128)S(1)}, f32[64,128]{1,0:T(8,128)S(1)}, u32[]{:S(2)}, u32[]{:S(2)}) collective-permute-start(f32[64,128]{1,0:T(8,128)S(1)} %step.10.cur), channel_id=1, source_target_pairs={{1,0},{2,1},{3,2},{4,3},{5,4},{6,5},{7,6},{0,7},{9,8},{10,9},{11,1... | collective-permute-start | bytes 98312 | tf_op jit(solution)/shard_map/ppermute | solution.py:112
  53.7 5.1 %collective-permute-start.12 = (f32[64,128]{1,0:T(8,128)S(1)}, f32[64,128]{1,0:T(8,128)S(1)}, u32[]{:S(2)}, u32[]{:S(2)}) collective-permute-start(f32[64,128]{1,0:T(8,128)S(1)} %step.10.cur), channel_id=1, source_target_pairs={{0,1},{1,2},{2,3},{3,4},{4,5},{5,6},{6,7},{7,0},{8,9},{9,10},{10,1... | collective-permute-start | bytes 98312 | tf_op jit(solution)/shard_map/ppermute | solution.py:111
  65.8 4.8 %collective-permute-start.18 = (f32[64,128]{1,0:T(8,128)S(1)}, f32[64,128]{1,0:T(8,128)S(1)}, u32[]{:S(2)}, u32[]{:S(2)}) collective-permute-start(f32[64,128]{1,0:T(8,128)S(1)} %step.11.cur), channel_id=1, source_target_pairs={{0,8},{8,16},{16,24},{24,0},{1,9},{9,17},{17,25},{25,1},{2,10},{10... | collective-permute-start | bytes 98312 | tf_op jit(solution)/shard_map/ppermute | solution.py:113
  65.8 4.8 %collective-permute-start.17 = (f32[64,128]{1,0:T(8,128)S(1)}, f32[64,128]{1,0:T(8,128)S(1)}, u32[]{:S(2)}, u32[]{:S(2)}) collective-permute-start(f32[64,128]{1,0:T(8,128)S(1)} %step.11.cur), channel_id=1, source_target_pairs={{1,0},{2,1},{3,2},{4,3},{5,4},{6,5},{7,6},{0,7},{9,8},{10,9},{11,1... | collective-permute-start | bytes 98312 | tf_op jit(solution)/shard_map/ppermute | solution.py:112
  65.8 5.1 %collective-permute-start.16 = (f32[64,128]{1,0:T(8,128)S(1)}, f32[64,128]{1,0:T(8,128)S(1)}, u32[]{:S(2)}, u32[]{:S(2)}) collective-permute-start(f32[64,128]{1,0:T(8,128)S(1)} %step.11.cur), channel_id=1, source_target_pairs={{0,1},{1,2},{2,3},{3,4},{4,5},{5,6},{6,7},{7,0},{8,9},{9,10},{10,1... | collective-permute-start | bytes 98312 | tf_op jit(solution)/shard_map/ppermute | solution.py:111
  77.9 4.8 %collective-permute-start.22 = (f32[64,128]{1,0:T(8,128)S(1)}, f32[64,128]{1,0:T(8,128)S(1)}, u32[]{:S(2)}, u32[]{:S(2)}) collective-permute-start(f32[64,128]{1,0:T(8,128)S(1)} %step.12.cur), channel_id=1, source_target_pairs={{0,8},{8,16},{16,24},{24,0},{1,9},{9,17},{17,25},{25,1},{2,10},{10... | collective-permute-start | bytes 98312 | tf_op jit(solution)/shard_map/ppermute | solution.py:113
  77.9 4.8 %collective-permute-start.21 = (f32[64,128]{1,0:T(8,128)S(1)}, f32[64,128]{1,0:T(8,128)S(1)}, u32[]{:S(2)}, u32[]{:S(2)}) collective-permute-start(f32[64,128]{1,0:T(8,128)S(1)} %step.12.cur), channel_id=1, source_target_pairs={{1,0},{2,1},{3,2},{4,3},{5,4},{6,5},{7,6},{0,7},{9,8},{10,9},{11,1... | collective-permute-start | bytes 98312 | tf_op jit(solution)/shard_map/ppermute | solution.py:112
  77.9 5.1 %collective-permute-start.20 = (f32[64,128]{1,0:T(8,128)S(1)}, f32[64,128]{1,0:T(8,128)S(1)}, u32[]{:S(2)}, u32[]{:S(2)}) collective-permute-start(f32[64,128]{1,0:T(8,128)S(1)} %step.12.cur), channel_id=1, source_target_pairs={{0,1},{1,2},{2,3},{3,4},{4,5},{5,6},{6,7},{7,0},{8,9},{9,10},{10,1... | collective-permute-start | bytes 98312 | tf_op jit(solution)/shard_map/ppermute | solution.py:111
  90.0 4.8 %collective-permute-start.26 = (f32[64,128]{1,0:T(8,128)S(1)}, f32[64,128]{1,0:T(8,128)S(1)}, u32[]{:S(2)}, u32[]{:S(2)}) collective-permute-start(f32[64,128]{1,0:T(8,128)S(1)} %step.13.cur), channel_id=1, source_target_pairs={{0,8},{8,16},{16,24},{24,0},{1,9},{9,17},{17,25},{25,1},{2,10},{10... | collective-permute-start | bytes 98312 | tf_op jit(solution)/shard_map/ppermute | solution.py:113
  90.0 4.8 %collective-permute-start.25 = (f32[64,128]{1,0:T(8,128)S(1)}, f32[64,128]{1,0:T(8,128)S(1)}, u32[]{:S(2)}, u32[]{:S(2)}) collective-permute-start(f32[64,128]{1,0:T(8,128)S(1)} %step.13.cur), channel_id=1, source_target_pairs={{1,0},{2,1},{3,2},{4,3},{5,4},{6,5},{7,6},{0,7},{9,8},{10,9},{11,1... | collective-permute-start | bytes 98312 | tf_op jit(solution)/shard_map/ppermute | solution.py:112
  90.0 5.1 %collective-permute-start.24 = (f32[64,128]{1,0:T(8,128)S(1)}, f32[64,128]{1,0:T(8,128)S(1)}, u32[]{:S(2)}, u32[]{:S(2)}) collective-permute-start(f32[64,128]{1,0:T(8,128)S(1)} %step.13.cur), channel_id=1, source_target_pairs={{0,1},{1,2},{2,3},{3,4},{4,5},{5,6},{6,7},{7,0},{8,9},{9,10},{10,1... | collective-permute-start | bytes 98312 | tf_op jit(solution)/shard_map/ppermute | solution.py:111
  102.1 5.1 %collective-permute-start.28 = (f32[64,128]{1,0:T(8,128)S(1)}, f32[64,128]{1,0:T(8,128)S(1)}, u32[]{:S(2)}, u32[]{:S(2)}) collective-permute-start(f32[64,128]{1,0:T(8,128)S(1)} %step.14.cur), channel_id=1, source_target_pairs={{0,1},{1,2},{2,3},{3,4},{4,5},{5,6},{6,7},{7,0},{8,9},{9,10},{10,1... | collective-permute-start | bytes 98312 | tf_op jit(solution)/shard_map/ppermute | solution.py:111
  (22 other events, 176.1 us)
where the time goes:
time: 135 us; the launch traced here: 134 us
  waiting for transfers between devices  45.8 us (34%)
  starting transfers between devices  36 us (27%)
  Pallas kernels  34.9 us (26%)
  local copies, waits for them, and re-layouts  15.7 us (12%)
    pallas_call x8, Pallas kernels, per_device(): pl.pallas_call(functools.partial(step_kernel, step=step, rows=rows, nslot...  31.8 us
    ppermute x8, starting transfers between devices, halos(): lax.ppermute(cur, 'group', gdown)  24 us
    ppermute x8, waiting for transfers between devices, halos(): lax.ppermute(cur, 'group', gup)  21.4 us
    unnamed x21, local copies, waits for them, and re-layouts  14.1 us
    ppermute x5, waiting for transfers between devices, sum_over(): x = x + lax.ppermute(x, axis, [(i, i ^ d) for i in range(n)])  12.6 us
    ppermute x8, waiting for transfers between devices, halos(): lax.ppermute(cur, 'group', gdown)  6.1 us
    ppermute x8, waiting for transfers between devices, halos(): lax.ppermute(cur, 'dom', up)  5.56 us
    ppermute x8, starting transfers between devices, halos(): lax.ppermute(cur, 'dom', down)  5.43 us
  transfers between devices with their start and end apart: 37, of which 26 were waited for; matrix products, arithmetic and copies ran while one was open for 2% of the time, Pallas kernels for 2%

commit v1 on v0

--- a/solution.py
+++ b/solution.py
@@ -6,7 +6,7 @@
 from jax.experimental.pallas import tpu as pltpu
 from jax.sharding import PartitionSpec as P
 
-def table_kernel(cols, live, need, tbl, *, rows, nslots, halo):
+def build_table(cols, live, need, tbl, rows, nslots, halo):
     far = 10 * rows
 
     def build(b, carry):
@@ -23,7 +23,26 @@
     lax.fori_loop(0, rows, build, 0)
 
 
-def step_kernel(tbl, shifts, cur, diag, h0, h1, h2, h3, a_ref, out, ext, halves, *, step, rows, nslots):
+def first_kernel(cols, live, need, shifts, cur, diag, h0, h1, h2, h3, a_hbm, out, a_vmem, tbl, ext, halves, sems, *, rows, nslots, halo):
+    def copy(g):
+        at = pl.ds(g * 2 * nslots, 2 * nslots)
+        return pltpu.make_async_copy(a_hbm.at[at], a_vmem.at[at], sems.at[g])
+
+    def start(g, carry):
+        copy(g).start()
+        return carry
+
+    lax.fori_loop(0, rows // 2, start, 0)
+    build_table(cols, live, need, tbl, rows, nslots, halo)
+    step_kernel(
+        tbl, shifts, cur, diag, h0, h1, h2, h3, a_vmem, out, ext, halves,
+        step=0, last=False, rows=rows, nslots=nslots, ready=lambda g: copy(g).wait(),
+    )
+
+
+def step_kernel(
+    tbl, shifts, cur, diag, h0, h1, h2, h3, a_ref, out, ext, halves, *, step, last, rows, nslots, ready=None
+):
     bs = ext.shape[1]
     half = bs // 2
     far = 10 * rows
@@ -45,6 +64,8 @@
             out[pl.ds(rows + at + u, 1), :] = sums[1:2, u * bs : (u + 1) * bs]
 
     def pair(g, carry):
+        if ready is not None:
+            ready(g)
         lane_sums(jnp.maximum(2 * g - 2, 0))
         for u in range(2):
             first = (2 * g + u) * nslots
@@ -53,10 +74,13 @@
                 at = tbl[first + s]
                 a = a_ref[first + s]
                 tp = a * ext[pl.ds(at, 1), :]
-                tr = a * ext[pl.ds(at + rows, 1), :]
                 ap = tp if ap is None else ap + tp
-                ar = tr if ar is None else ar + tr
-            both = jnp.where(low, ap + pltpu.roll(ap, half, 1), ar + pltpu.roll(ar, half, 1))
+                if not last:
+                    tr = a * ext[pl.ds(at + rows, 1), :]
+                    ar = tr if ar is None else ar + tr
+            both = ap + pltpu.roll(ap, half, 1)
+            if not last:
+                both = jnp.where(low, both, ar + pltpu.roll(ar, half, 1))
             hi = both.astype(jnp.bfloat16)
             lo = (both - hi.astype(jnp.float32)).astype(jnp.bfloat16)
             halves[u * bs : (u + 1) * bs, 0:bs] = hi
@@ -76,8 +100,13 @@
         return lax.psum(x, axis)
     d = 1
     while d < n:
-        x = x + lax.ppermute(x, axis, [(i, i ^ d) for i in range(n)])
-        d *= 2
+        wide = min(8, n // d)
+        parts = [lax.ppermute(x, axis, [(i, i ^ (d * k)) for i in range(n)]) for k in range(1, wide)]
+        parts = [x] + parts
+        while len(parts) > 1:
+            parts = [parts[k] + parts[k + 1] for k in range(0, len(parts), 2)]
+        x = parts[0]
+        d *= wide
     return x
 
 
@@ -91,16 +120,8 @@
     vmem = pl.BlockSpec(memory_space=pltpu.VMEM)
     field = jax.ShapeDtypeStruct((2 * rows, bs), f32)
     scratch = [pltpu.VMEM((10 * rows + rows + 8, bs), f32), pltpu.VMEM((2 * bs, 2 * bs), jnp.bfloat16)]
-    params = pltpu.CompilerParams(vmem_limit_bytes=24 * 1024 * 1024)
-    a_flat = block_values.reshape(rows * nslots, bs, bs)
-    tbl = pl.pallas_call(
-        functools.partial(table_kernel, rows=rows, nslots=nslots, halo=halo),
-        out_shape=jax.ShapeDtypeStruct((rows * nslots,), jnp.int32),
-        in_specs=[smem, smem, smem],
-        out_specs=smem,
-        name="table",
-    )(block_cols, live_slots, needed[0])
-
+    params = pltpu.CompilerParams(vmem_limit_bytes=4 * 1024 * 1024)
+    a_flat = pltpu.with_memory_space_constraint(block_values.reshape(rows * nslots, bs, bs), pltpu.HBM)
     def halos(cur):
         nd, ng = lax.axis_size("dom"), lax.axis_size("group")
         up = [(i, (i + 1) % nd) for i in range(nd)]
@@ -118,15 +139,30 @@
     fields = [cur]
     for step in range(depth):
         h = halos(cur)
-        cur = pl.pallas_call(
-            functools.partial(step_kernel, step=step, rows=rows, nslots=nslots),
-            out_shape=field,
-            in_specs=[smem, smem] + [vmem] * 7,
-            out_specs=vmem,
-            scratch_shapes=scratch,
-            compiler_params=params,
-            name="step",
-        )(tbl, shifts, cur, diag_shift, *h, a_flat)
+        if step == 0:
+            cur, a_vmem, tbl = pl.pallas_call(
+                functools.partial(first_kernel, rows=rows, nslots=nslots, halo=halo),
+                out_shape=(
+                    field,
+                    pltpu.VMEM((rows * nslots, bs, bs), f32),
+                    jax.ShapeDtypeStruct((rows * nslots,), jnp.int32),
+                ),
+                in_specs=[smem] * 4 + [vmem] * 6 + [pl.BlockSpec(memory_space=pltpu.HBM)],
+                out_specs=(vmem, vmem, smem),
+                scratch_shapes=scratch + [pltpu.SemaphoreType.DMA((rows // 2,))],
+                compiler_params=params,
+                name="first",
+            )(block_cols, live_slots, needed[0], shifts, cur, diag_shift, *h, a_flat)
+        else:
+            cur = pl.pallas_call(
+                functools.partial(step_kernel, step=step, last=step == depth - 1, rows=rows, nslots=nslots),
+                out_shape=field,
+                in_specs=[smem, smem] + [vmem] * 7,
+                out_specs=vmem,
+                scratch_shapes=scratch,
+                compiler_params=params,
+                name="step",
+            )(tbl, shifts, cur, diag_shift, *h, a_vmem)
         fields.append(cur)
     both = jnp.stack(fields).reshape(depth + 1, 2, rows, bs)
     basis = jnp.concatenate([both[:, 0], both[:depth, 1]], axis=0)

time: 135 us -> 130 us (0.963)
  starting transfers between devices: 36 us -> 42.5 us
  waiting for transfers between devices: 45.8 us -> 41 us
  local copies, waits for them, and re-layouts: 15.7 us -> 11.1 us
  Pallas kernels: 34.9 us -> 33 us
    ppermute x5 -> x10, starting transfers between devices: 3.42 us -> 11.8 us  [sum_over(): lax.ppermute(x, axis, [(i, i ^ d * k) for i in range(n)])]
    ppermute x5 -> x10, waiting for transfers between devices: 12.6 us -> 4.65 us  [sum_over(): lax.ppermute(x, axis, [(i, i ^ d * k) for i in range(n)])]
    unnamed x21 -> x19, local copies, waits for them, and re-layouts: 14.1 us -> 9.57 us
    ppermute x8, starting transfers between devices: 5.43 us -> 2.78 us  [halos(): lax.ppermute(cur, 'dom', down)]
    ppermute x8, waiting for transfers between devices: 21.4 us -> 23.8 us  [halos(): lax.ppermute(cur, 'group', gup)]
    pallas_call x9 -> x8, Pallas kernels: 34.9 us -> 33 us  [the longest x7 26.7 us: per_device(): pl.pallas_call(functools.partial(step_kernel, step=step, last=step == dep...]
  transfers between devices with their start and end apart: 37 -> 42, of which waited for: 26 -> 28; matrix products, arithmetic and copies ran while one was open for 2% -> 2% of each run, Pallas kernels for 2% -> 0%
where the time goes in v1:
time: 130 us; the launch traced here: 129 us
  starting transfers between devices  42.5 us (33%)
  waiting for transfers between devices  41 us (32%)
  Pallas kernels  33 us (25%)
  local copies, waits for them, and re-layouts  11.1 us (9%)
    pallas_call x7, Pallas kernels, per_device(): pl.pallas_call(functools.partial(step_kernel, step=step, last=step == dep...  26.7 us
    ppermute x8, starting transfers between devices, halos(): lax.ppermute(cur, 'group', gdown)  24.3 us
    ppermute x8, waiting for transfers between devices, halos(): lax.ppermute(cur, 'group', gup)  23.8 us
    ppermute x10, starting transfers between devices, sum_over(): lax.ppermute(x, axis, [(i, i ^ d * k) for i in range(n)])  11.8 us
    unnamed x19, local copies, waits for them, and re-layouts  9.57 us
    ppermute x8, waiting for transfers between devices, halos(): lax.ppermute(cur, 'group', gdown)  7.18 us
    pallas_call x1, Pallas kernels, per_device(): pl.pallas_call(functools.partial(first_kernel, rows=rows, nslots=nslots,...  6.32 us
    ppermute x8, waiting for transfers between devices, halos(): lax.ppermute(cur, 'dom', up)  5.38 us
  transfers between devices with their start and end apart: 42, of which 28 were waited for; matrix products, arithmetic and copies ran while one was open for 2% of the time, Pallas kernels for 0%

profile of v1, /device:TPU:0, one launch (start us, length us, event | category | flops | bytes accessed | tf_op | source)
XLA Modules:
  0.0 129.5 jit_solution(10674302932538598683)
XLA Ops:
  2.1 3.9 %collective-permute-start.3 = (f32[64,128]{1,0:T(8,128)S(1)}, f32[64,128]{1,0:T(8,128)S(1)}, u32[]{:S(2)}, u32[]{:S(2)}) collective-permute-start(f32[64,128]{1,0:T(8,128)S(1)} %constant_dynamic-update-slice_fusion.cur), channel_id=1, source_target_pairs={{8,0},{16,8},{24,16},{0,24},{9,1},{17,9},{25,17},{1,25},{10,2},{18... | collective-permute-start | bytes 98312 | tf_op jit(solution)/shard_map/ppermute | solution.py:135
  10.8 3.1 %collective-permute-done.h0 = f32[64,128]{1,0:T(8,128)S(1)} collective-permute-done((f32[64,128]{1,0:T(8,128)S(1)}, f32[64,128]{1,0:T(8,128)S(1)}, u32[]{:S(2)}, u32[]{:S(2)}) %collective-permute-start) | collective-permute-done | bytes 32800 | tf_op jit(solution)/shard_map/ppermute | solution.py:132
  16.6 6.3 %first.1 = (f32[64,128]{1,0:T(8,128)S(1)}, f32[192,128,128]{2,1,0:T(8,128)S(1)}, s32[192]{0:T(256)S(1)}) custom-call(s32[32,6]{1,0:T(8,128)S(1)} %copy.10.cols, s32[32]{0:T(128)S(1)} %copy-done.7, s32[4,16]{1,0:T(4,128)S(1)} %bitcast.60, f32[8]{0:T(128)S(1)} %copy-done.4, f32[64,128]{1,0:T(8,128)S(1)} %constant_dynamic-update-slice_fusion.cur, ...), custom_call_target="tpu_custom_call" | custom-call | tf_op jit(solution)/shard_map/first/pallas_call | solution.py:143
  27.2 3.2 %collective-permute-done.6.h2 = f32[64,128]{1,0:T(8,128)S(1)} collective-permute-done((f32[64,128]{1,0:T(8,128)S(1)}, f32[64,128]{1,0:T(8,128)S(1)}, u32[]{:S(2)}, u32[]{:S(2)}) %collective-permute-start.6) | collective-permute-done | bytes 32800 | tf_op jit(solution)/shard_map/ppermute | solution.py:134
  30.8 3.8 %step.7.cur = f32[64,128]{1,0:T(8,128)S(1)} custom-call(s32[192]{0:T(256)S(1)} %get-tuple-element.6.tbl, f32[8]{0:T(128)S(1)} %copy-done.4, f32[64,128]{1,0:T(8,128)S(1)} %get-tuple-element.5.cur, f32[32,128]{1,0:T(8,128)S(1)} %copy-done.2, f32[64,128]{1,0:T(8,128)S(1)} %collective-permute-done.4.h0, f32[64,128]{1,0:T(8,128)S(1)} %collective-permute-done.5.h1, ...), custom_call_target="tpu_custom_call" | custom-call | tf_op jit(solution)/shard_map/step/pallas_call | solution.py:157
  34.6 3.0 %collective-permute-start.11 = (f32[64,128]{1,0:T(8,128)S(1)}, f32[64,128]{1,0:T(8,128)S(1)}, u32[]{:S(2)}, u32[]{:S(2)}) collective-permute-start(f32[64,128]{1,0:T(8,128)S(1)} %step.7.cur), channel_id=1, source_target_pairs={{8,0},{16,8},{24,16},{0,24},{9,1},{17,9},{25,17},{1,25},{10,2},{18... | collective-permute-start | bytes 98312 | tf_op jit(solution)/shard_map/ppermute | solution.py:135
  39.2 3.2 %collective-permute-done.10.h2 = f32[64,128]{1,0:T(8,128)S(1)} collective-permute-done((f32[64,128]{1,0:T(8,128)S(1)}, f32[64,128]{1,0:T(8,128)S(1)}, u32[]{:S(2)}, u32[]{:S(2)}) %collective-permute-start.10) | collective-permute-done | bytes 32800 | tf_op jit(solution)/shard_map/ppermute | solution.py:134
  42.7 3.8 %step.8.cur = f32[64,128]{1,0:T(8,128)S(1)} custom-call(s32[192]{0:T(256)S(1)} %get-tuple-element.6.tbl, f32[8]{0:T(128)S(1)} %copy-done.4, f32[64,128]{1,0:T(8,128)S(1)} %step.7.cur, f32[32,128]{1,0:T(8,128)S(1)} %copy-done.2, f32[64,128]{1,0:T(8,128)S(1)} %collective-permute-done.8.h0, f32[64,128]{1,0:T(8,128)S(1)} %collective-permute-done.9.h1, ...), custom_call_target="tpu_custom_call" | custom-call | tf_op jit(solution)/shard_map/step/pallas_call | solution.py:157
  46.5 3.0 %collective-permute-start.15 = (f32[64,128]{1,0:T(8,128)S(1)}, f32[64,128]{1,0:T(8,128)S(1)}, u32[]{:S(2)}, u32[]{:S(2)}) collective-permute-start(f32[64,128]{1,0:T(8,128)S(1)} %step.8.cur), channel_id=1, source_target_pairs={{8,0},{16,8},{24,16},{0,24},{9,1},{17,9},{25,17},{1,25},{10,2},{18... | collective-permute-start | bytes 98312 | tf_op jit(solution)/shard_map/ppermute | solution.py:135
  51.1 3.2 %collective-permute-done.14.h2 = f32[64,128]{1,0:T(8,128)S(1)} collective-permute-done((f32[64,128]{1,0:T(8,128)S(1)}, f32[64,128]{1,0:T(8,128)S(1)}, u32[]{:S(2)}, u32[]{:S(2)}) %collective-permute-start.14) | collective-permute-done | bytes 32800 | tf_op jit(solution)/shard_map/ppermute | solution.py:134
  54.6 3.8 %step.9.cur = f32[64,128]{1,0:T(8,128)S(1)} custom-call(s32[192]{0:T(256)S(1)} %get-tuple-element.6.tbl, f32[8]{0:T(128)S(1)} %copy-done.4, f32[64,128]{1,0:T(8,128)S(1)} %step.8.cur, f32[32,128]{1,0:T(8,128)S(1)} %copy-done.2, f32[64,128]{1,0:T(8,128)S(1)} %collective-permute-done.12.h0, f32[64,128]{1,0:T(8,128)S(1)} %collective-permute-done.13.h1, ...), custom_call_target="tpu_custom_call" | custom-call | tf_op jit(solution)/shard_map/step/pallas_call | solution.py:157
  58.5 3.0 %collective-permute-start.19 = (f32[64,128]{1,0:T(8,128)S(1)}, f32[64,128]{1,0:T(8,128)S(1)}, u32[]{:S(2)}, u32[]{:S(2)}) collective-permute-start(f32[64,128]{1,0:T(8,128)S(1)} %step.9.cur), channel_id=1, source_target_pairs={{8,0},{16,8},{24,16},{0,24},{9,1},{17,9},{25,17},{1,25},{10,2},{18... | collective-permute-start | bytes 98312 | tf_op jit(solution)/shard_map/ppermute | solution.py:135
  63.0 3.2 %collective-permute-done.18.h2 = f32[64,128]{1,0:T(8,128)S(1)} collective-permute-done((f32[64,128]{1,0:T(8,128)S(1)}, f32[64,128]{1,0:T(8,128)S(1)}, u32[]{:S(2)}, u32[]{:S(2)}) %collective-permute-start.18) | collective-permute-done | bytes 32800 | tf_op jit(solution)/shard_map/ppermute | solution.py:134
  66.6 3.8 %step.10.cur = f32[64,128]{1,0:T(8,128)S(1)} custom-call(s32[192]{0:T(256)S(1)} %get-tuple-element.6.tbl, f32[8]{0:T(128)S(1)} %copy-done.4, f32[64,128]{1,0:T(8,128)S(1)} %step.9.cur, f32[32,128]{1,0:T(8,128)S(1)} %copy-done.2, f32[64,128]{1,0:T(8,128)S(1)} %collective-permute-done.16.h0, f32[64,128]{1,0:T(8,128)S(1)} %collective-permute-done.17.h1, ...), custom_call_target="tpu_custom_call" | custom-call | tf_op jit(solution)/shard_map/step/pallas_call | solution.py:157
  70.4 3.0 %collective-permute-start.23 = (f32[64,128]{1,0:T(8,128)S(1)}, f32[64,128]{1,0:T(8,128)S(1)}, u32[]{:S(2)}, u32[]{:S(2)}) collective-permute-start(f32[64,128]{1,0:T(8,128)S(1)} %step.10.cur), channel_id=1, source_target_pairs={{8,0},{16,8},{24,16},{0,24},{9,1},{17,9},{25,17},{1,25},{10,2},{18... | collective-permute-start | bytes 98312 | tf_op jit(solution)/shard_map/ppermute | solution.py:135
  75.0 3.2 %collective-permute-done.22.h2 = f32[64,128]{1,0:T(8,128)S(1)} collective-permute-done((f32[64,128]{1,0:T(8,128)S(1)}, f32[64,128]{1,0:T(8,128)S(1)}, u32[]{:S(2)}, u32[]{:S(2)}) %collective-permute-start.22) | collective-permute-done | bytes 32800 | tf_op jit(solution)/shard_map/ppermute | solution.py:134
  78.6 3.8 %step.11.cur = f32[64,128]{1,0:T(8,128)S(1)} custom-call(s32[192]{0:T(256)S(1)} %get-tuple-element.6.tbl, f32[8]{0:T(128)S(1)} %copy-done.4, f32[64,128]{1,0:T(8,128)S(1)} %step.10.cur, f32[32,128]{1,0:T(8,128)S(1)} %copy-done.2, f32[64,128]{1,0:T(8,128)S(1)} %collective-permute-done.20.h0, f32[64,128]{1,0:T(8,128)S(1)} %collective-permute-done.21.h1, ...), custom_call_target="tpu_custom_call" | custom-call | tf_op jit(solution)/shard_map/step/pallas_call | solution.py:157
  86.9 3.2 %collective-permute-done.26.h2 = f32[64,128]{1,0:T(8,128)S(1)} collective-permute-done((f32[64,128]{1,0:T(8,128)S(1)}, f32[64,128]{1,0:T(8,128)S(1)}, u32[]{:S(2)}, u32[]{:S(2)}) %collective-permute-start.26) | collective-permute-done | bytes 32800 | tf_op jit(solution)/shard_map/ppermute | solution.py:134
  90.5 3.8 %step.12.cur = f32[64,128]{1,0:T(8,128)S(1)} custom-call(s32[192]{0:T(256)S(1)} %get-tuple-element.6.tbl, f32[8]{0:T(128)S(1)} %copy-done.4, f32[64,128]{1,0:T(8,128)S(1)} %step.11.cur, f32[32,128]{1,0:T(8,128)S(1)} %copy-done.2, f32[64,128]{1,0:T(8,128)S(1)} %collective-permute-done.24.h0, f32[64,128]{1,0:T(8,128)S(1)} %collective-permute-done.25.h1, ...), custom_call_target="tpu_custom_call" | custom-call | tf_op jit(solution)/shard_map/step/pallas_call | solution.py:157
  98.9 3.2 %collective-permute-done.30.h2 = f32[64,128]{1,0:T(8,128)S(1)} collective-permute-done((f32[64,128]{1,0:T(8,128)S(1)}, f32[64,128]{1,0:T(8,128)S(1)}, u32[]{:S(2)}, u32[]{:S(2)}) %collective-permute-start.30) | collective-permute-done | bytes 32800 | tf_op jit(solution)/shard_map/ppermute | solution.py:134
  102.4 4.6 %copy-done.1 = f32[192,128,128]{2,1,0:T(8,128)S(1)} copy-done((f32[192,128,128]{2,1,0:T(8,128)S(1)}, f32[192,128,128]{2,1,0:T(8,128)}, u32[]{:S(2)}) %copy-start.1) | copy-done | bytes 12582936
  107.0 3.7 %step.13 = f32[64,128]{1,0:T(8,128)S(1)} custom-call(s32[192]{0:T(256)S(1)} %get-tuple-element.6.tbl, f32[8]{0:T(128)S(1)} %copy-done.5, f32[64,128]{1,0:T(8,128)S(1)} %step.12.cur, f32[32,128]{1,0:T(8,128)S(1)} %copy-done.3, f32[64,128]{1,0:T(8,128)S(1)} %collective-permute-done.28.h0, f32[64,128]{1,0:T(8,128)S(1)} %collective-permute-done.29.h1, ...), custom_call_target="tpu_custom_call" | custom-call | tf_op jit(solution)/shard_map/step/pallas_call | solution.py:157
  111.8 6.0 %collective-permute-start.35 = (f32[17,17]{1,0:T(8,128)S(1)}, f32[17,17]{1,0:T(8,128)S(1)}, u32[]{:S(2)}, u32[]{:S(2)}) collective-permute-start(f32[17,17]{1,0:T(8,128)S(1)} %convolution_bitcast_fusion), channel_id=1, source_target_pairs={{0,4},{1,5},{2,6},{3,7},{4,0},{5,1},{6,2},{7,3},{8,12},{9,13},{10,... | collective-permute-start | bytes 3476 | tf_op jit(solution)/shard_map/ppermute | solution.py:104
  121.6 3.1 %collective-permute-start.41 = (f32[17,17]{1,0:T(8,128)S(1)}, f32[17,17]{1,0:T(8,128)S(1)}, u32[]{:S(2)}, u32[]{:S(2)}) collective-permute-start(f32[17,17]{1,0:T(8,128)S(1)} %add_add_fusion), channel_id=1, source_target_pairs={{0,24},{8,16},{16,8},{24,0},{1,25},{9,17},{17,9},{25,1},{2,26},{10... | collective-permute-start | bytes 3476 | tf_op jit(solution)/shard_map/ppermute | solution.py:104
  (96 shorter events, 40.7 us)
Async XLA Ops:
  2.1 7.5 %collective-permute-start.3 = (f32[64,128]{1,0:T(8,128)S(1)}, f32[64,128]{1,0:T(8,128)S(1)}, u32[]{:S(2)}, u32[]{:S(2)}) collective-permute-start(f32[64,128]{1,0:T(8,128)S(1)} %constant_dynamic-update-slice_fusion.cur), channel_id=1, source_target_pairs={{8,0},{16,8},{24,16},{0,24},{9,1},{17,9},{25,17},{1,25},{10,2},{18... | collective-permute-start | bytes 98312 | tf_op jit(solution)/shard_map/ppermute | solution.py:135
  6.0 4.8 %collective-permute-start.2 = (f32[64,128]{1,0:T(8,128)S(1)}, f32[64,128]{1,0:T(8,128)S(1)}, u32[]{:S(2)}, u32[]{:S(2)}) collective-permute-start(f32[64,128]{1,0:T(8,128)S(1)} %constant_dynamic-update-slice_fusion.cur), channel_id=1, source_target_pairs={{0,8},{8,16},{16,24},{24,0},{1,9},{9,17},{17,25},{25,1},{2,10},{10... | collective-permute-start | bytes 98312 | tf_op jit(solution)/shard_map/ppermute | solution.py:134
  6.0 4.8 %collective-permute-start.1 = (f32[64,128]{1,0:T(8,128)S(1)}, f32[64,128]{1,0:T(8,128)S(1)}, u32[]{:S(2)}, u32[]{:S(2)}) collective-permute-start(f32[64,128]{1,0:T(8,128)S(1)} %constant_dynamic-update-slice_fusion.cur), channel_id=1, source_target_pairs={{1,0},{2,1},{3,2},{4,3},{5,4},{6,5},{7,6},{0,7},{9,8},{10,9},{11,1... | collective-permute-start | bytes 98312 | tf_op jit(solution)/shard_map/ppermute | solution.py:133
  8.8 5.1 %collective-permute-start = (f32[64,128]{1,0:T(8,128)S(1)}, f32[64,128]{1,0:T(8,128)S(1)}, u32[]{:S(2)}, u32[]{:S(2)}) collective-permute-start(f32[64,128]{1,0:T(8,128)S(1)} %constant_dynamic-update-slice_fusion.cur), channel_id=1, source_target_pairs={{0,1},{1,2},{2,3},{3,4},{4,5},{5,6},{6,7},{7,0},{8,9},{9,10},{10,1... | collective-permute-start | bytes 98312 | tf_op jit(solution)/shard_map/ppermute | solution.py:132
  25.6 4.8 %collective-permute-start.6 = (f32[64,128]{1,0:T(8,128)S(1)}, f32[64,128]{1,0:T(8,128)S(1)}, u32[]{:S(2)}, u32[]{:S(2)}) collective-permute-start(f32[64,128]{1,0:T(8,128)S(1)} %get-tuple-element.5.cur), channel_id=1, source_target_pairs={{0,8},{8,16},{16,24},{24,0},{1,9},{9,17},{17,25},{25,1},{2,10},{10... | collective-permute-start | bytes 98312 | tf_op jit(solution)/shard_map/ppermute | solution.py:134
  25.6 4.8 %collective-permute-start.5 = (f32[64,128]{1,0:T(8,128)S(1)}, f32[64,128]{1,0:T(8,128)S(1)}, u32[]{:S(2)}, u32[]{:S(2)}) collective-permute-start(f32[64,128]{1,0:T(8,128)S(1)} %get-tuple-element.5.cur), channel_id=1, source_target_pairs={{1,0},{2,1},{3,2},{4,3},{5,4},{6,5},{7,6},{0,7},{9,8},{10,9},{11,1... | collective-permute-start | bytes 98312 | tf_op jit(solution)/shard_map/ppermute | solution.py:133
  25.6 5.1 %collective-permute-start.4 = (f32[64,128]{1,0:T(8,128)S(1)}, f32[64,128]{1,0:T(8,128)S(1)}, u32[]{:S(2)}, u32[]{:S(2)}) collective-permute-start(f32[64,128]{1,0:T(8,128)S(1)} %get-tuple-element.5.cur), channel_id=1, source_target_pairs={{0,1},{1,2},{2,3},{3,4},{4,5},{5,6},{6,7},{7,0},{8,9},{9,10},{10,1... | collective-permute-start | bytes 98312 | tf_op jit(solution)/shard_map/ppermute | solution.py:132
  37.6 4.8 %collective-permute-start.10 = (f32[64,128]{1,0:T(8,128)S(1)}, f32[64,128]{1,0:T(8,128)S(1)}, u32[]{:S(2)}, u32[]{:S(2)}) collective-permute-start(f32[64,128]{1,0:T(8,128)S(1)} %step.7.cur), channel_id=1, source_target_pairs={{0,8},{8,16},{16,24},{24,0},{1,9},{9,17},{17,25},{25,1},{2,10},{10... | collective-permute-start | bytes 98312 | tf_op jit(solution)/shard_map/ppermute | solution.py:134
  37.6 4.8 %collective-permute-start.9 = (f32[64,128]{1,0:T(8,128)S(1)}, f32[64,128]{1,0:T(8,128)S(1)}, u32[]{:S(2)}, u32[]{:S(2)}) collective-permute-start(f32[64,128]{1,0:T(8,128)S(1)} %step.7.cur), channel_id=1, source_target_pairs={{1,0},{2,1},{3,2},{4,3},{5,4},{6,5},{7,6},{0,7},{9,8},{10,9},{11,1... | collective-permute-start | bytes 98312 | tf_op jit(solution)/shard_map/ppermute | solution.py:133
  37.6 5.1 %collective-permute-start.8 = (f32[64,128]{1,0:T(8,128)S(1)}, f32[64,128]{1,0:T(8,128)S(1)}, u32[]{:S(2)}, u32[]{:S(2)}) collective-permute-start(f32[64,128]{1,0:T(8,128)S(1)} %step.7.cur), channel_id=1, source_target_pairs={{0,1},{1,2},{2,3},{3,4},{4,5},{5,6},{6,7},{7,0},{8,9},{9,10},{10,1... | collective-permute-start | bytes 98312 | tf_op jit(solution)/shard_map/ppermute | solution.py:132
  49.5 4.8 %collective-permute-start.14 = (f32[64,128]{1,0:T(8,128)S(1)}, f32[64,128]{1,0:T(8,128)S(1)}, u32[]{:S(2)}, u32[]{:S(2)}) collective-permute-start(f32[64,128]{1,0:T(8,128)S(1)} %step.8.cur), channel_id=1, source_target_pairs={{0,8},{8,16},{16,24},{24,0},{1,9},{9,17},{17,25},{25,1},{2,10},{10... | collective-permute-start | bytes 98312 | tf_op jit(solution)/shard_map/ppermute | solution.py:134
  49.5 4.8 %collective-permute-start.13 = (f32[64,128]{1,0:T(8,128)S(1)}, f32[64,128]{1,0:T(8,128)S(1)}, u32[]{:S(2)}, u32[]{:S(2)}) collective-permute-start(f32[64,128]{1,0:T(8,128)S(1)} %step.8.cur), channel_id=1, source_target_pairs={{1,0},{2,1},{3,2},{4,3},{5,4},{6,5},{7,6},{0,7},{9,8},{10,9},{11,1... | collective-permute-start | bytes 98312 | tf_op jit(solution)/shard_map/ppermute | solution.py:133
  49.5 5.1 %collective-permute-start.12 = (f32[64,128]{1,0:T(8,128)S(1)}, f32[64,128]{1,0:T(8,128)S(1)}, u32[]{:S(2)}, u32[]{:S(2)}) collective-permute-start(f32[64,128]{1,0:T(8,128)S(1)} %step.8.cur), channel_id=1, source_target_pairs={{0,1},{1,2},{2,3},{3,4},{4,5},{5,6},{6,7},{7,0},{8,9},{9,10},{10,1... | collective-permute-start | bytes 98312 | tf_op jit(solution)/shard_map/ppermute | solution.py:132
  61.4 4.8 %collective-permute-start.18 = (f32[64,128]{1,0:T(8,128)S(1)}, f32[64,128]{1,0:T(8,128)S(1)}, u32[]{:S(2)}, u32[]{:S(2)}) collective-permute-start(f32[64,128]{1,0:T(8,128)S(1)} %step.9.cur), channel_id=1, source_target_pairs={{0,8},{8,16},{16,24},{24,0},{1,9},{9,17},{17,25},{25,1},{2,10},{10... | collective-permute-start | bytes 98312 | tf_op jit(solution)/shard_map/ppermute | solution.py:134
  61.4 4.8 %collective-permute-start.17 = (f32[64,128]{1,0:T(8,128)S(1)}, f32[64,128]{1,0:T(8,128)S(1)}, u32[]{:S(2)}, u32[]{:S(2)}) collective-permute-start(f32[64,128]{1,0:T(8,128)S(1)} %step.9.cur), channel_id=1, source_target_pairs={{1,0},{2,1},{3,2},{4,3},{5,4},{6,5},{7,6},{0,7},{9,8},{10,9},{11,1... | collective-permute-start | bytes 98312 | tf_op jit(solution)/shard_map/ppermute | solution.py:133
  61.4 5.1 %collective-permute-start.16 = (f32[64,128]{1,0:T(8,128)S(1)}, f32[64,128]{1,0:T(8,128)S(1)}, u32[]{:S(2)}, u32[]{:S(2)}) collective-permute-start(f32[64,128]{1,0:T(8,128)S(1)} %step.9.cur), channel_id=1, source_target_pairs={{0,1},{1,2},{2,3},{3,4},{4,5},{5,6},{6,7},{7,0},{8,9},{9,10},{10,1... | collective-permute-start | bytes 98312 | tf_op jit(solution)/shard_map/ppermute | solution.py:132
  73.4 4.8 %collective-permute-start.22 = (f32[64,128]{1,0:T(8,128)S(1)}, f32[64,128]{1,0:T(8,128)S(1)}, u32[]{:S(2)}, u32[]{:S(2)}) collective-permute-start(f32[64,128]{1,0:T(8,128)S(1)} %step.10.cur), channel_id=1, source_target_pairs={{0,8},{8,16},{16,24},{24,0},{1,9},{9,17},{17,25},{25,1},{2,10},{10... | collective-permute-start | bytes 98312 | tf_op jit(solution)/shard_map/ppermute | solution.py:134
  73.4 5.1 %collective-permute-start.20 = (f32[64,128]{1,0:T(8,128)S(1)}, f32[64,128]{1,0:T(8,128)S(1)}, u32[]{:S(2)}, u32[]{:S(2)}) collective-permute-start(f32[64,128]{1,0:T(8,128)S(1)} %step.10.cur), channel_id=1, source_target_pairs={{0,1},{1,2},{2,3},{3,4},{4,5},{5,6},{6,7},{7,0},{8,9},{9,10},{10,1... | collective-permute-start | bytes 98312 | tf_op jit(solution)/shard_map/ppermute | solution.py:132
  85.3 5.1 %collective-permute-start.24 = (f32[64,128]{1,0:T(8,128)S(1)}, f32[64,128]{1,0:T(8,128)S(1)}, u32[]{:S(2)}, u32[]{:S(2)}) collective-permute-start(f32[64,128]{1,0:T(8,128)S(1)} %step.11.cur), channel_id=1, source_target_pairs={{0,1},{1,2},{2,3},{3,4},{4,5},{5,6},{6,7},{7,0},{8,9},{9,10},{10,1... | collective-permute-start | bytes 98312 | tf_op jit(solution)/shard_map/ppermute | solution.py:132
  97.3 5.1 %collective-permute-start.28 = (f32[64,128]{1,0:T(8,128)S(1)}, f32[64,128]{1,0:T(8,128)S(1)}, u32[]{:S(2)}, u32[]{:S(2)}) collective-permute-start(f32[64,128]{1,0:T(8,128)S(1)} %step.12.cur), channel_id=1, source_target_pairs={{0,1},{1,2},{2,3},{3,4},{4,5},{5,6},{6,7},{7,0},{8,9},{9,10},{10,1... | collective-permute-start | bytes 98312 | tf_op jit(solution)/shard_map/ppermute | solution.py:132
  111.6 6.2 %collective-permute-start.38 = (f32[17,17]{1,0:T(8,128)S(1)}, f32[17,17]{1,0:T(8,128)S(1)}, u32[]{:S(2)}, u32[]{:S(2)}) collective-permute-start(f32[17,17]{1,0:T(8,128)S(1)} %convolution_bitcast_fusion), channel_id=1, source_target_pairs={{0,7},{1,6},{2,5},{3,4},{4,3},{5,2},{6,1},{7,0},{8,15},{9,14},{10,... | collective-permute-start | bytes 3476 | tf_op jit(solution)/shard_map/ppermute | solution.py:104
  111.8 6.0 %collective-permute-start.37 = (f32[17,17]{1,0:T(8,128)S(1)}, f32[17,17]{1,0:T(8,128)S(1)}, u32[]{:S(2)}, u32[]{:S(2)}) collective-permute-start(f32[17,17]{1,0:T(8,128)S(1)} %convolution_bitcast_fusion), channel_id=1, source_target_pairs={{0,6},{1,7},{2,4},{3,5},{4,2},{5,3},{6,0},{7,1},{8,14},{9,15},{10,... | collective-permute-start | bytes 3476 | tf_op jit(solution)/shard_map/ppermute | solution.py:104
  111.8 7.9 %collective-permute-start.36 = (f32[17,17]{1,0:T(8,128)S(1)}, f32[17,17]{1,0:T(8,128)S(1)}, u32[]{:S(2)}, u32[]{:S(2)}) collective-permute-start(f32[17,17]{1,0:T(8,128)S(1)} %convolution_bitcast_fusion), channel_id=1, source_target_pairs={{0,5},{1,4},{2,7},{3,6},{4,1},{5,0},{6,3},{7,2},{8,13},{9,12},{10,... | collective-permute-start | bytes 3476 | tf_op jit(solution)/shard_map/ppermute | solution.py:104
  111.8 7.9 %collective-permute-start.35 = (f32[17,17]{1,0:T(8,128)S(1)}, f32[17,17]{1,0:T(8,128)S(1)}, u32[]{:S(2)}, u32[]{:S(2)}) collective-permute-start(f32[17,17]{1,0:T(8,128)S(1)} %convolution_bitcast_fusion), channel_id=1, source_target_pairs={{0,4},{1,5},{2,6},{3,7},{4,0},{5,1},{6,2},{7,3},{8,12},{9,13},{10,... | collective-permute-start | bytes 3476 | tf_op jit(solution)/shard_map/ppermute | solution.py:104
  (26 other events, 217.2 us)

commit v2 on v1

--- a/solution.py
+++ b/solution.py
@@ -164,6 +164,7 @@
                 name="step",
             )(tbl, shifts, cur, diag_shift, *h, a_vmem)
         fields.append(cur)
+    fields = lax.optimization_barrier(fields)
     both = jnp.stack(fields).reshape(depth + 1, 2, rows, bs)
     basis = jnp.concatenate([both[:, 0], both[:depth, 1]], axis=0)
     total_cells = rows * bs * lax.axis_size("group") * lax.axis_size("dom")

time: 130 us -> 126 us (0.969)
  local copies, waits for them, and re-layouts: 11.1 us -> 6.54 us
    unnamed x19 -> x11, local copies, waits for them, and re-layouts: 9.57 us -> 4.96 us
  transfers between devices with their start and end apart: 42 -> 42, of which waited for: 28 -> 28; matrix products, arithmetic and copies ran while one was open for 2% -> 1% of each run, Pallas kernels for 0% -> 0%
where the time goes in v2:
time: 126 us; the launch traced here: 125 us
  starting transfers between devices  42.4 us (34%)
  waiting for transfers between devices  41.2 us (33%)
  Pallas kernels  33 us (26%)
  local copies, waits for them, and re-layouts  6.54 us (5%)
    pallas_call x7, Pallas kernels, per_device(): pl.pallas_call(functools.partial(step_kernel, step=step, last=step == dep...  26.6 us
    ppermute x8, starting transfers between devices, halos(): lax.ppermute(cur, 'group', gdown)  24.4 us
    ppermute x8, waiting for transfers between devices, halos(): lax.ppermute(cur, 'group', gup)  23.8 us
    ppermute x10, starting transfers between devices, sum_over(): lax.ppermute(x, axis, [(i, i ^ d * k) for i in range(n)])  11.7 us
    ppermute x8, waiting for transfers between devices, halos(): lax.ppermute(cur, 'group', gdown)  7.59 us
    pallas_call x1, Pallas kernels, per_device(): pl.pallas_call(functools.partial(first_kernel, rows=rows, nslots=nslots,...  6.33 us
    ppermute x8, waiting for transfers between devices, halos(): lax.ppermute(cur, 'dom', up)  5.38 us
    unnamed x11, local copies, waits for them, and re-layouts  4.96 us
  transfers between devices with their start and end apart: 42, of which 28 were waited for; matrix products, arithmetic and copies ran while one was open for 1% of the time, Pallas kernels for 0%

profile of v2, /device:TPU:0, one launch (start us, length us, event | category | flops | bytes accessed | tf_op | source)
XLA Modules:
  0.0 125.0 jit_solution(9762867252101564202)
XLA Ops:
  2.1 3.9 %collective-permute-start.3 = (f32[64,128]{1,0:T(8,128)S(1)}, f32[64,128]{1,0:T(8,128)S(1)}, u32[]{:S(2)}, u32[]{:S(2)}) collective-permute-start(f32[64,128]{1,0:T(8,128)S(1)} %constant_dynamic-update-slice_fusion.cur), channel_id=1, source_target_pairs={{8,0},{16,8},{24,16},{0,24},{9,1},{17,9},{25,17},{1,25},{10,2},{18... | collective-permute-start | bytes 98312 | tf_op jit(solution)/shard_map/ppermute | solution.py:135
  10.8 3.1 %collective-permute-done.h0 = f32[64,128]{1,0:T(8,128)S(1)} collective-permute-done((f32[64,128]{1,0:T(8,128)S(1)}, f32[64,128]{1,0:T(8,128)S(1)}, u32[]{:S(2)}, u32[]{:S(2)}) %collective-permute-start) | collective-permute-done | bytes 32800 | tf_op jit(solution)/shard_map/ppermute | solution.py:132
  16.6 6.3 %first.1 = (f32[64,128]{1,0:T(8,128)S(1)}, f32[192,128,128]{2,1,0:T(8,128)S(1)}, s32[192]{0:T(256)S(1)}) custom-call(s32[32,6]{1,0:T(8,128)S(1)} %copy.10.cols, s32[32]{0:T(128)S(1)} %copy-done.3, s32[4,16]{1,0:T(4,128)S(1)} %bitcast.60, f32[8]{0:T(128)S(1)} %copy-done.1, f32[64,128]{1,0:T(8,128)S(1)} %constant_dynamic-update-slice_fusion.cur, ...), custom_call_target="tpu_custom_call" | custom-call | tf_op jit(solution)/shard_map/first/pallas_call | solution.py:143
  27.2 3.2 %collective-permute-done.6.h2 = f32[64,128]{1,0:T(8,128)S(1)} collective-permute-done((f32[64,128]{1,0:T(8,128)S(1)}, f32[64,128]{1,0:T(8,128)S(1)}, u32[]{:S(2)}, u32[]{:S(2)}) %collective-permute-start.6) | collective-permute-done | bytes 32800 | tf_op jit(solution)/shard_map/ppermute | solution.py:134
  30.8 3.8 %step.7.cur = f32[64,128]{1,0:T(8,128)S(1)} custom-call(s32[192]{0:T(256)S(1)} %get-tuple-element.15.tbl, f32[8]{0:T(128)S(1)} %copy-done.1, f32[64,128]{1,0:T(8,128)S(1)} %get-tuple-element.18.cur, f32[32,128]{1,0:T(8,128)S(1)} %copy-done, f32[64,128]{1,0:T(8,128)S(1)} %collective-permute-done.4.h0, f32[64,128]{1,0:T(8,128)S(1)} %collective-permute-done.5.h1, ...), custom_call_target="tpu_custom_call" | custom-call | tf_op jit(solution)/shard_map/step/pallas_call | solution.py:157
  34.6 3.0 %collective-permute-start.11 = (f32[64,128]{1,0:T(8,128)S(1)}, f32[64,128]{1,0:T(8,128)S(1)}, u32[]{:S(2)}, u32[]{:S(2)}) collective-permute-start(f32[64,128]{1,0:T(8,128)S(1)} %step.7.cur), channel_id=1, source_target_pairs={{8,0},{16,8},{24,16},{0,24},{9,1},{17,9},{25,17},{1,25},{10,2},{18... | collective-permute-start | bytes 98312 | tf_op jit(solution)/shard_map/ppermute | solution.py:135
  39.2 3.2 %collective-permute-done.10.h2 = f32[64,128]{1,0:T(8,128)S(1)} collective-permute-done((f32[64,128]{1,0:T(8,128)S(1)}, f32[64,128]{1,0:T(8,128)S(1)}, u32[]{:S(2)}, u32[]{:S(2)}) %collective-permute-start.10) | collective-permute-done | bytes 32800 | tf_op jit(solution)/shard_map/ppermute | solution.py:134
  42.7 3.8 %step.8.cur = f32[64,128]{1,0:T(8,128)S(1)} custom-call(s32[192]{0:T(256)S(1)} %get-tuple-element.15.tbl, f32[8]{0:T(128)S(1)} %copy-done.1, f32[64,128]{1,0:T(8,128)S(1)} %step.7.cur, f32[32,128]{1,0:T(8,128)S(1)} %copy-done, f32[64,128]{1,0:T(8,128)S(1)} %collective-permute-done.8.h0, f32[64,128]{1,0:T(8,128)S(1)} %collective-permute-done.9.h1, ...), custom_call_target="tpu_custom_call" | custom-call | tf_op jit(solution)/shard_map/step/pallas_call | solution.py:157
  46.6 3.0 %collective-permute-start.15 = (f32[64,128]{1,0:T(8,128)S(1)}, f32[64,128]{1,0:T(8,128)S(1)}, u32[]{:S(2)}, u32[]{:S(2)}) collective-permute-start(f32[64,128]{1,0:T(8,128)S(1)} %step.8.cur), channel_id=1, source_target_pairs={{8,0},{16,8},{24,16},{0,24},{9,1},{17,9},{25,17},{1,25},{10,2},{18... | collective-permute-start | bytes 98312 | tf_op jit(solution)/shard_map/ppermute | solution.py:135
  51.1 3.2 %collective-permute-done.14.h2 = f32[64,128]{1,0:T(8,128)S(1)} collective-permute-done((f32[64,128]{1,0:T(8,128)S(1)}, f32[64,128]{1,0:T(8,128)S(1)}, u32[]{:S(2)}, u32[]{:S(2)}) %collective-permute-start.14) | collective-permute-done | bytes 32800 | tf_op jit(solution)/shard_map/ppermute | solution.py:134
  54.7 3.8 %step.9.cur = f32[64,128]{1,0:T(8,128)S(1)} custom-call(s32[192]{0:T(256)S(1)} %get-tuple-element.15.tbl, f32[8]{0:T(128)S(1)} %copy-done.1, f32[64,128]{1,0:T(8,128)S(1)} %step.8.cur, f32[32,128]{1,0:T(8,128)S(1)} %copy-done, f32[64,128]{1,0:T(8,128)S(1)} %collective-permute-done.12.h0, f32[64,128]{1,0:T(8,128)S(1)} %collective-permute-done.13.h1, ...), custom_call_target="tpu_custom_call" | custom-call | tf_op jit(solution)/shard_map/step/pallas_call | solution.py:157
  58.5 3.0 %collective-permute-start.19 = (f32[64,128]{1,0:T(8,128)S(1)}, f32[64,128]{1,0:T(8,128)S(1)}, u32[]{:S(2)}, u32[]{:S(2)}) collective-permute-start(f32[64,128]{1,0:T(8,128)S(1)} %step.9.cur), channel_id=1, source_target_pairs={{8,0},{16,8},{24,16},{0,24},{9,1},{17,9},{25,17},{1,25},{10,2},{18... | collective-permute-start | bytes 98312 | tf_op jit(solution)/shard_map/ppermute | solution.py:135
  63.0 3.2 %collective-permute-done.18.h2 = f32[64,128]{1,0:T(8,128)S(1)} collective-permute-done((f32[64,128]{1,0:T(8,128)S(1)}, f32[64,128]{1,0:T(8,128)S(1)}, u32[]{:S(2)}, u32[]{:S(2)}) %collective-permute-start.18) | collective-permute-done | bytes 32800 | tf_op jit(solution)/shard_map/ppermute | solution.py:134
  66.6 3.8 %step.10.cur = f32[64,128]{1,0:T(8,128)S(1)} custom-call(s32[192]{0:T(256)S(1)} %get-tuple-element.15.tbl, f32[8]{0:T(128)S(1)} %copy-done.1, f32[64,128]{1,0:T(8,128)S(1)} %step.9.cur, f32[32,128]{1,0:T(8,128)S(1)} %copy-done, f32[64,128]{1,0:T(8,128)S(1)} %collective-permute-done.16.h0, f32[64,128]{1,0:T(8,128)S(1)} %collective-permute-done.17.h1, ...), custom_call_target="tpu_custom_call" | custom-call | tf_op jit(solution)/shard_map/step/pallas_call | solution.py:157
  70.4 3.0 %collective-permute-start.23 = (f32[64,128]{1,0:T(8,128)S(1)}, f32[64,128]{1,0:T(8,128)S(1)}, u32[]{:S(2)}, u32[]{:S(2)}) collective-permute-start(f32[64,128]{1,0:T(8,128)S(1)} %step.10.cur), channel_id=1, source_target_pairs={{8,0},{16,8},{24,16},{0,24},{9,1},{17,9},{25,17},{1,25},{10,2},{18... | collective-permute-start | bytes 98312 | tf_op jit(solution)/shard_map/ppermute | solution.py:135
  75.0 3.2 %collective-permute-done.22.h2 = f32[64,128]{1,0:T(8,128)S(1)} collective-permute-done((f32[64,128]{1,0:T(8,128)S(1)}, f32[64,128]{1,0:T(8,128)S(1)}, u32[]{:S(2)}, u32[]{:S(2)}) %collective-permute-start.22) | collective-permute-done | bytes 32800 | tf_op jit(solution)/shard_map/ppermute | solution.py:134
  78.5 3.8 %step.11.cur = f32[64,128]{1,0:T(8,128)S(1)} custom-call(s32[192]{0:T(256)S(1)} %get-tuple-element.15.tbl, f32[8]{0:T(128)S(1)} %copy-done.1, f32[64,128]{1,0:T(8,128)S(1)} %step.10.cur, f32[32,128]{1,0:T(8,128)S(1)} %copy-done, f32[64,128]{1,0:T(8,128)S(1)} %collective-permute-done.20.h0, f32[64,128]{1,0:T(8,128)S(1)} %collective-permute-done.21.h1, ...), custom_call_target="tpu_custom_call" | custom-call | tf_op jit(solution)/shard_map/step/pallas_call | solution.py:157
  86.9 3.2 %collective-permute-done.26.h2 = f32[64,128]{1,0:T(8,128)S(1)} collective-permute-done((f32[64,128]{1,0:T(8,128)S(1)}, f32[64,128]{1,0:T(8,128)S(1)}, u32[]{:S(2)}, u32[]{:S(2)}) %collective-permute-start.26) | collective-permute-done | bytes 32800 | tf_op jit(solution)/shard_map/ppermute | solution.py:134
  90.5 3.8 %step.12.cur = f32[64,128]{1,0:T(8,128)S(1)} custom-call(s32[192]{0:T(256)S(1)} %get-tuple-element.15.tbl, f32[8]{0:T(128)S(1)} %copy-done.1, f32[64,128]{1,0:T(8,128)S(1)} %step.11.cur, f32[32,128]{1,0:T(8,128)S(1)} %copy-done, f32[64,128]{1,0:T(8,128)S(1)} %collective-permute-done.24.h0, f32[64,128]{1,0:T(8,128)S(1)} %collective-permute-done.25.h1, ...), custom_call_target="tpu_custom_call" | custom-call | tf_op jit(solution)/shard_map/step/pallas_call | solution.py:157
  94.3 3.0 %collective-permute-start.31 = (f32[64,128]{1,0:T(8,128)S(1)}, f32[64,128]{1,0:T(8,128)S(1)}, u32[]{:S(2)}, u32[]{:S(2)}) collective-permute-start(f32[64,128]{1,0:T(8,128)S(1)} %step.12.cur), channel_id=1, source_target_pairs={{8,0},{16,8},{24,16},{0,24},{9,1},{17,9},{25,17},{1,25},{10,2},{18... | collective-permute-start | bytes 98312 | tf_op jit(solution)/shard_map/ppermute | solution.py:135
  98.9 3.2 %collective-permute-done.30.h2 = f32[64,128]{1,0:T(8,128)S(1)} collective-permute-done((f32[64,128]{1,0:T(8,128)S(1)}, f32[64,128]{1,0:T(8,128)S(1)}, u32[]{:S(2)}, u32[]{:S(2)}) %collective-permute-start.30) | collective-permute-done | bytes 32800 | tf_op jit(solution)/shard_map/ppermute | solution.py:134
  102.4 3.6 %step.13 = f32[64,128]{1,0:T(8,128)S(1)} custom-call(s32[192]{0:T(256)S(1)} %get-tuple-element.15.tbl, f32[8]{0:T(128)S(1)} %copy-done.1, f32[64,128]{1,0:T(8,128)S(1)} %step.12.cur, f32[32,128]{1,0:T(8,128)S(1)} %copy-done, f32[64,128]{1,0:T(8,128)S(1)} %collective-permute-done.28.h0, f32[64,128]{1,0:T(8,128)S(1)} %collective-permute-done.29.h1, ...), custom_call_target="tpu_custom_call" | custom-call | tf_op jit(solution)/shard_map/step/pallas_call | solution.py:157
  107.6 6.0 %collective-permute-start.35 = (f32[17,17]{1,0:T(8,128)S(1)}, f32[17,17]{1,0:T(8,128)S(1)}, u32[]{:S(2)}, u32[]{:S(2)}) collective-permute-start(f32[17,17]{1,0:T(8,128)S(1)} %convolution_bitcast_fusion), channel_id=1, source_target_pairs={{0,4},{1,5},{2,6},{3,7},{4,0},{5,1},{6,2},{7,3},{8,12},{9,13},{10,... | collective-permute-start | bytes 3476 | tf_op jit(solution)/shard_map/ppermute | solution.py:104
  117.3 3.0 %collective-permute-start.41 = (f32[17,17]{1,0:T(8,128)S(1)}, f32[17,17]{1,0:T(8,128)S(1)}, u32[]{:S(2)}, u32[]{:S(2)}) collective-permute-start(f32[17,17]{1,0:T(8,128)S(1)} %add_add_fusion), channel_id=1, source_target_pairs={{0,24},{8,16},{16,8},{24,0},{1,25},{9,17},{17,9},{25,1},{2,26},{10... | collective-permute-start | bytes 3476 | tf_op jit(solution)/shard_map/ppermute | solution.py:104
  (88 shorter events, 38.0 us)
Async XLA Ops:
  2.1 7.5 %collective-permute-start.3 = (f32[64,128]{1,0:T(8,128)S(1)}, f32[64,128]{1,0:T(8,128)S(1)}, u32[]{:S(2)}, u32[]{:S(2)}) collective-permute-start(f32[64,128]{1,0:T(8,128)S(1)} %constant_dynamic-update-slice_fusion.cur), channel_id=1, source_target_pairs={{8,0},{16,8},{24,16},{0,24},{9,1},{17,9},{25,17},{1,25},{10,2},{18... | collective-permute-start | bytes 98312 | tf_op jit(solution)/shard_map/ppermute | solution.py:135
  6.0 4.8 %collective-permute-start.2 = (f32[64,128]{1,0:T(8,128)S(1)}, f32[64,128]{1,0:T(8,128)S(1)}, u32[]{:S(2)}, u32[]{:S(2)}) collective-permute-start(f32[64,128]{1,0:T(8,128)S(1)} %constant_dynamic-update-slice_fusion.cur), channel_id=1, source_target_pairs={{0,8},{8,16},{16,24},{24,0},{1,9},{9,17},{17,25},{25,1},{2,10},{10... | collective-permute-start | bytes 98312 | tf_op jit(solution)/shard_map/ppermute | solution.py:134
  6.0 4.8 %collective-permute-start.1 = (f32[64,128]{1,0:T(8,128)S(1)}, f32[64,128]{1,0:T(8,128)S(1)}, u32[]{:S(2)}, u32[]{:S(2)}) collective-permute-start(f32[64,128]{1,0:T(8,128)S(1)} %constant_dynamic-update-slice_fusion.cur), channel_id=1, source_target_pairs={{1,0},{2,1},{3,2},{4,3},{5,4},{6,5},{7,6},{0,7},{9,8},{10,9},{11,1... | collective-permute-start | bytes 98312 | tf_op jit(solution)/shard_map/ppermute | solution.py:133
  8.8 5.1 %collective-permute-start = (f32[64,128]{1,0:T(8,128)S(1)}, f32[64,128]{1,0:T(8,128)S(1)}, u32[]{:S(2)}, u32[]{:S(2)}) collective-permute-start(f32[64,128]{1,0:T(8,128)S(1)} %constant_dynamic-update-slice_fusion.cur), channel_id=1, source_target_pairs={{0,1},{1,2},{2,3},{3,4},{4,5},{5,6},{6,7},{7,0},{8,9},{9,10},{10,1... | collective-permute-start | bytes 98312 | tf_op jit(solution)/shard_map/ppermute | solution.py:132
  25.6 4.8 %collective-permute-start.6 = (f32[64,128]{1,0:T(8,128)S(1)}, f32[64,128]{1,0:T(8,128)S(1)}, u32[]{:S(2)}, u32[]{:S(2)}) collective-permute-start(f32[64,128]{1,0:T(8,128)S(1)} %get-tuple-element.18.cur), channel_id=1, source_target_pairs={{0,8},{8,16},{16,24},{24,0},{1,9},{9,17},{17,25},{25,1},{2,10},{10... | collective-permute-start | bytes 98312 | tf_op jit(solution)/shard_map/ppermute | solution.py:134
  25.6 4.8 %collective-permute-start.5 = (f32[64,128]{1,0:T(8,128)S(1)}, f32[64,128]{1,0:T(8,128)S(1)}, u32[]{:S(2)}, u32[]{:S(2)}) collective-permute-start(f32[64,128]{1,0:T(8,128)S(1)} %get-tuple-element.18.cur), channel_id=1, source_target_pairs={{1,0},{2,1},{3,2},{4,3},{5,4},{6,5},{7,6},{0,7},{9,8},{10,9},{11,1... | collective-permute-start | bytes 98312 | tf_op jit(solution)/shard_map/ppermute | solution.py:133
  25.6 5.1 %collective-permute-start.4 = (f32[64,128]{1,0:T(8,128)S(1)}, f32[64,128]{1,0:T(8,128)S(1)}, u32[]{:S(2)}, u32[]{:S(2)}) collective-permute-start(f32[64,128]{1,0:T(8,128)S(1)} %get-tuple-element.18.cur), channel_id=1, source_target_pairs={{0,1},{1,2},{2,3},{3,4},{4,5},{5,6},{6,7},{7,0},{8,9},{9,10},{10,1... | collective-permute-start | bytes 98312 | tf_op jit(solution)/shard_map/ppermute | solution.py:132
  37.6 4.8 %collective-permute-start.10 = (f32[64,128]{1,0:T(8,128)S(1)}, f32[64,128]{1,0:T(8,128)S(1)}, u32[]{:S(2)}, u32[]{:S(2)}) collective-permute-start(f32[64,128]{1,0:T(8,128)S(1)} %step.7.cur), channel_id=1, source_target_pairs={{0,8},{8,16},{16,24},{24,0},{1,9},{9,17},{17,25},{25,1},{2,10},{10... | collective-permute-start | bytes 98312 | tf_op jit(solution)/shard_map/ppermute | solution.py:134
  37.6 4.8 %collective-permute-start.9 = (f32[64,128]{1,0:T(8,128)S(1)}, f32[64,128]{1,0:T(8,128)S(1)}, u32[]{:S(2)}, u32[]{:S(2)}) collective-permute-start(f32[64,128]{1,0:T(8,128)S(1)} %step.7.cur), channel_id=1, source_target_pairs={{1,0},{2,1},{3,2},{4,3},{5,4},{6,5},{7,6},{0,7},{9,8},{10,9},{11,1... | collective-permute-start | bytes 98312 | tf_op jit(solution)/shard_map/ppermute | solution.py:133
  37.6 5.1 %collective-permute-start.8 = (f32[64,128]{1,0:T(8,128)S(1)}, f32[64,128]{1,0:T(8,128)S(1)}, u32[]{:S(2)}, u32[]{:S(2)}) collective-permute-start(f32[64,128]{1,0:T(8,128)S(1)} %step.7.cur), channel_id=1, source_target_pairs={{0,1},{1,2},{2,3},{3,4},{4,5},{5,6},{6,7},{7,0},{8,9},{9,10},{10,1... | collective-permute-start | bytes 98312 | tf_op jit(solution)/shard_map/ppermute | solution.py:132
  49.5 4.8 %collective-permute-start.14 = (f32[64,128]{1,0:T(8,128)S(1)}, f32[64,128]{1,0:T(8,128)S(1)}, u32[]{:S(2)}, u32[]{:S(2)}) collective-permute-start(f32[64,128]{1,0:T(8,128)S(1)} %step.8.cur), channel_id=1, source_target_pairs={{0,8},{8,16},{16,24},{24,0},{1,9},{9,17},{17,25},{25,1},{2,10},{10... | collective-permute-start | bytes 98312 | tf_op jit(solution)/shard_map/ppermute | solution.py:134
  49.5 4.8 %collective-permute-start.13 = (f32[64,128]{1,0:T(8,128)S(1)}, f32[64,128]{1,0:T(8,128)S(1)}, u32[]{:S(2)}, u32[]{:S(2)}) collective-permute-start(f32[64,128]{1,0:T(8,128)S(1)} %step.8.cur), channel_id=1, source_target_pairs={{1,0},{2,1},{3,2},{4,3},{5,4},{6,5},{7,6},{0,7},{9,8},{10,9},{11,1... | collective-permute-start | bytes 98312 | tf_op jit(solution)/shard_map/ppermute | solution.py:133
  49.5 5.1 %collective-permute-start.12 = (f32[64,128]{1,0:T(8,128)S(1)}, f32[64,128]{1,0:T(8,128)S(1)}, u32[]{:S(2)}, u32[]{:S(2)}) collective-permute-start(f32[64,128]{1,0:T(8,128)S(1)} %step.8.cur), channel_id=1, source_target_pairs={{0,1},{1,2},{2,3},{3,4},{4,5},{5,6},{6,7},{7,0},{8,9},{9,10},{10,1... | collective-permute-start | bytes 98312 | tf_op jit(solution)/shard_map/ppermute | solution.py:132
  61.5 4.8 %collective-permute-start.18 = (f32[64,128]{1,0:T(8,128)S(1)}, f32[64,128]{1,0:T(8,128)S(1)}, u32[]{:S(2)}, u32[]{:S(2)}) collective-permute-start(f32[64,128]{1,0:T(8,128)S(1)} %step.9.cur), channel_id=1, source_target_pairs={{0,8},{8,16},{16,24},{24,0},{1,9},{9,17},{17,25},{25,1},{2,10},{10... | collective-permute-start | bytes 98312 | tf_op jit(solution)/shard_map/ppermute | solution.py:134
  61.5 4.8 %collective-permute-start.17 = (f32[64,128]{1,0:T(8,128)S(1)}, f32[64,128]{1,0:T(8,128)S(1)}, u32[]{:S(2)}, u32[]{:S(2)}) collective-permute-start(f32[64,128]{1,0:T(8,128)S(1)} %step.9.cur), channel_id=1, source_target_pairs={{1,0},{2,1},{3,2},{4,3},{5,4},{6,5},{7,6},{0,7},{9,8},{10,9},{11,1... | collective-permute-start | bytes 98312 | tf_op jit(solution)/shard_map/ppermute | solution.py:133
  61.5 5.1 %collective-permute-start.16 = (f32[64,128]{1,0:T(8,128)S(1)}, f32[64,128]{1,0:T(8,128)S(1)}, u32[]{:S(2)}, u32[]{:S(2)}) collective-permute-start(f32[64,128]{1,0:T(8,128)S(1)} %step.9.cur), channel_id=1, source_target_pairs={{0,1},{1,2},{2,3},{3,4},{4,5},{5,6},{6,7},{7,0},{8,9},{9,10},{10,1... | collective-permute-start | bytes 98312 | tf_op jit(solution)/shard_map/ppermute | solution.py:132
  73.4 5.1 %collective-permute-start.20 = (f32[64,128]{1,0:T(8,128)S(1)}, f32[64,128]{1,0:T(8,128)S(1)}, u32[]{:S(2)}, u32[]{:S(2)}) collective-permute-start(f32[64,128]{1,0:T(8,128)S(1)} %step.10.cur), channel_id=1, source_target_pairs={{0,1},{1,2},{2,3},{3,4},{4,5},{5,6},{6,7},{7,0},{8,9},{9,10},{10,1... | collective-permute-start | bytes 98312 | tf_op jit(solution)/shard_map/ppermute | solution.py:132
  85.3 4.8 %collective-permute-start.25 = (f32[64,128]{1,0:T(8,128)S(1)}, f32[64,128]{1,0:T(8,128)S(1)}, u32[]{:S(2)}, u32[]{:S(2)}) collective-permute-start(f32[64,128]{1,0:T(8,128)S(1)} %step.11.cur), channel_id=1, source_target_pairs={{1,0},{2,1},{3,2},{4,3},{5,4},{6,5},{7,6},{0,7},{9,8},{10,9},{11,1... | collective-permute-start | bytes 98312 | tf_op jit(solution)/shard_map/ppermute | solution.py:133
  85.3 5.1 %collective-permute-start.24 = (f32[64,128]{1,0:T(8,128)S(1)}, f32[64,128]{1,0:T(8,128)S(1)}, u32[]{:S(2)}, u32[]{:S(2)}) collective-permute-start(f32[64,128]{1,0:T(8,128)S(1)} %step.11.cur), channel_id=1, source_target_pairs={{0,1},{1,2},{2,3},{3,4},{4,5},{5,6},{6,7},{7,0},{8,9},{9,10},{10,1... | collective-permute-start | bytes 98312 | tf_op jit(solution)/shard_map/ppermute | solution.py:132
  97.3 5.1 %collective-permute-start.28 = (f32[64,128]{1,0:T(8,128)S(1)}, f32[64,128]{1,0:T(8,128)S(1)}, u32[]{:S(2)}, u32[]{:S(2)}) collective-permute-start(f32[64,128]{1,0:T(8,128)S(1)} %step.12.cur), channel_id=1, source_target_pairs={{0,1},{1,2},{2,3},{3,4},{4,5},{5,6},{6,7},{7,0},{8,9},{9,10},{10,1... | collective-permute-start | bytes 98312 | tf_op jit(solution)/shard_map/ppermute | solution.py:132
  107.4 6.2 %collective-permute-start.38 = (f32[17,17]{1,0:T(8,128)S(1)}, f32[17,17]{1,0:T(8,128)S(1)}, u32[]{:S(2)}, u32[]{:S(2)}) collective-permute-start(f32[17,17]{1,0:T(8,128)S(1)} %convolution_bitcast_fusion), channel_id=1, source_target_pairs={{0,7},{1,6},{2,5},{3,4},{4,3},{5,2},{6,1},{7,0},{8,15},{9,14},{10,... | collective-permute-start | bytes 3476 | tf_op jit(solution)/shard_map/ppermute | solution.py:104
  107.6 6.0 %collective-permute-start.37 = (f32[17,17]{1,0:T(8,128)S(1)}, f32[17,17]{1,0:T(8,128)S(1)}, u32[]{:S(2)}, u32[]{:S(2)}) collective-permute-start(f32[17,17]{1,0:T(8,128)S(1)} %convolution_bitcast_fusion), channel_id=1, source_target_pairs={{0,6},{1,7},{2,4},{3,5},{4,2},{5,3},{6,0},{7,1},{8,14},{9,15},{10,... | collective-permute-start | bytes 3476 | tf_op jit(solution)/shard_map/ppermute | solution.py:104
  107.6 7.9 %collective-permute-start.36 = (f32[17,17]{1,0:T(8,128)S(1)}, f32[17,17]{1,0:T(8,128)S(1)}, u32[]{:S(2)}, u32[]{:S(2)}) collective-permute-start(f32[17,17]{1,0:T(8,128)S(1)} %convolution_bitcast_fusion), channel_id=1, source_target_pairs={{0,5},{1,4},{2,7},{3,6},{4,1},{5,0},{6,3},{7,2},{8,13},{9,12},{10,... | collective-permute-start | bytes 3476 | tf_op jit(solution)/shard_map/ppermute | solution.py:104
  107.6 7.9 %collective-permute-start.35 = (f32[17,17]{1,0:T(8,128)S(1)}, f32[17,17]{1,0:T(8,128)S(1)}, u32[]{:S(2)}, u32[]{:S(2)}) collective-permute-start(f32[17,17]{1,0:T(8,128)S(1)} %convolution_bitcast_fusion), channel_id=1, source_target_pairs={{0,4},{1,5},{2,6},{3,7},{4,0},{5,1},{6,2},{7,3},{8,12},{9,13},{10,... | collective-permute-start | bytes 3476 | tf_op jit(solution)/shard_map/ppermute | solution.py:104
  (22 other events, 81.0 us)
